TPU v7x, 128 devices: a whole 4x4x4 slice. The times are simulated.
128 devices in a mesh: aa: 16 (over z_hi, x, core), ba: 8 (over z_lo, y).
Axes of the slice: x: 4, y: 4, z: 4 (z_hi: 2, z_lo: 2; z = z_hi * 2 + z_lo), core: 2. Of those that a mesh axis runs over, the one named last changes fastest.
Arguments:
- cotangent: bfloat16 [1, 20, 64, 64, 2048], P(None, None, 'aa', 'ba'), may hold values from -6 to 6
- pre_activations: bfloat16 [2, 1, 20, 64, 64, 2048], P(None, None, None, 'aa', 'ba'), may hold values from -6 to 6
- spectral_weights: bfloat16 [2, 2, 20, 20, 24, 6912], P(None, None, None, None, 'ba', 'aa'), may hold values from -6 to 6
- skip_weights: bfloat16 [2, 20, 20], replicated, may hold values from -1.25 to 1.25
- lift_weights: float32 [20], replicated, may hold values from -1.25 to 1.25
Outputs:
- perm_grad: float32 [1, 64, 64, 2048], P(None, 'aa', 'ba')
All inputs are finite; a program needn't handle non-finite values.
Results may differ from a plain program's by a relative error of at most 0.023.
Values may be sent and summed in bfloat16 or wider, within the bound.
A program may use at most 192 MiB of HBM per device.

v0:
```python
import functools
import math

import jax
import jax.numpy as jnp
import numpy as np
from jax import lax
from jax.experimental import pallas as pl
from jax.experimental.pallas import tpu as pltpu
from jax.sharding import PartitionSpec as P

C = 20
NZT = 2048
NA = 16
NB = 8
NG = 3
GC = 7
LM = 36
SCALE_ZT = 1.0 / NZT
BF = jnp.bfloat16
F32 = jnp.float32
INV_SQRT2 = 1.0 / math.sqrt(2.0)
INV_SQRT2PI = 1.0 / math.sqrt(2.0 * math.pi)


def freq(count):
    j = np.arange(count)
    return np.where(j < count // 2, j, j - count)


def plane_table():
    joint = np.arange(24 * 12)
    kz = freq(24)[joint // 12]
    kt = joint % 12
    cell = np.arange(NZT)
    turns = (kz[None, :] * (cell[:, None] // 32) * 32 + kt[None, :] * (cell[:, None] % 32) * 64) % NZT
    angle = 2.0 * np.pi / NZT * turns
    table = np.zeros((NZT, 768))
    owner, local = joint // 18, joint % 18
    column = 128 * (owner // 3) + LM * (owner % 3) + 2 * local
    table[:, column] = np.cos(angle)
    table[:, column + 1] = -np.sin(angle)
    return table


def line_angle():
    return 2.0 * np.pi / 64 * ((freq(24)[:, None] * np.arange(64)[None, :]) % 64)


def x_table():
    angle = line_angle()
    out = np.zeros((2, NB, 4, 8, 64, 8))
    for y in range(8):
        out[0, :, :3, y, :, y] = np.cos(angle).reshape(NB, 3, 64)
        out[1, :, :3, y, :, y] = np.sin(angle).reshape(NB, 3, 64)
    return out.reshape(2, 256, 512)


def y_table():
    angle = line_angle().reshape(24, NB, 8)
    out = np.zeros((2, 80, NB, 4, 8))
    for k in range(3):
        out[0, 24 * k : 24 * k + 24, :, k] = np.cos(angle)
        out[1, 24 * k : 24 * k + 24, :, k] = np.sin(angle)
    return out.reshape(2, 80, 256)


def y_back_table():
    wide = np.zeros((2, 256, 128))
    wide[:, :, :80] = y_table().transpose(0, 2, 1) / 64
    return wide


def swap(values):
    even = lax.broadcasted_iota(jnp.int32, (values.shape[0], 128), 1) % 2 == 0
    parts = []
    for t in range(values.shape[1] // 128):
        part = values[:, 128 * t : 128 * t + 128]
        parts.append(jnp.where(even, pltpu.roll(part, 127, 1), -pltpu.roll(part, 1, 1)))
    return parts[0] if len(parts) == 1 else jnp.concatenate(parts, 1)


def dot(a, b):
    return jnp.dot(a, b, preferred_element_type=F32)


def dot_nt(a, b):
    return lax.dot_general(a, b, (((1,), (1,)), ((), ())), preferred_element_type=F32)


def slope_of(v):
    normal_cdf = 0.5 + 0.5 * lax.erf(v * INV_SQRT2)
    return normal_cdf + v * (jnp.exp(-0.5 * v * v) * INV_SQRT2PI)


def loop(count, body):
    lax.fori_loop(0, count, lambda i, carry: (body(i), carry)[1], 0)


def kernel(
    cot_h, pre_h, wts_h, skip_ref, lift_ref, plane_h, xf_h, xb_h, yf_ref, yb_ref, out_ref,
    cot, pre, wts, plane, xf, xb, g1, g0, slope0, tbuf, bx, kron,
    s1, r1, s2, r2, s3, r3, s4, r4, t1, q1, t2, q2, t3, q3, t4, q4,
    q, sm, mm, mg, mt, weff, fold, fa, vv, mt0, bx0,
    in_sem, send_sem, recv_sem,
):
    me_a = lax.axis_index("aa")
    me_b = lax.axis_index("ba")
    lane = lax.broadcasted_iota(jnp.int32, (8, 128), 1)

    def lanes(rows):
        return lax.broadcasted_iota(jnp.int32, (rows, 128), 1)

    sizes = [min(GC, C - GC * g) for g in range(NG)]
    loads = []
    for g in range(NG):
        part = pl.ds(GC * g, sizes[g])
        loads.append(pltpu.make_async_copy(cot_h.at[part], cot.at[part], in_sem.at[2 * g]))
        loads.append(pltpu.make_async_copy(pre_h.at[1, part], pre.at[1, part], in_sem.at[2 * g + 1]))
    load_plane = pltpu.make_async_copy(plane_h, plane, in_sem.at[6])
    load_pre0 = pltpu.make_async_copy(pre_h.at[0], pre.at[0], in_sem.at[7])
    load_xf = pltpu.make_async_copy(xf_h, xf, in_sem.at[8])
    load_xb = pltpu.make_async_copy(xb_h, xb, in_sem.at[9])
    load_w1 = pltpu.make_async_copy(wts_h.at[1], wts.at[1, :, :, pl.ds(0, C)], in_sem.at[10])
    load_w0 = pltpu.make_async_copy(wts_h.at[0], wts.at[0, :, :, pl.ds(0, C)], in_sem.at[11])
    loads[0].start()
    loads[1].start()
    load_plane.start()
    for copy in loads[2:]:
        copy.start()
    load_xf.start()
    load_pre0.start()
    load_w1.start()
    load_xb.start()
    load_w0.start()

    barrier = pltpu.get_barrier_semaphore()

    def greet_a(d):
        peer = lax.rem(me_a + d + 1, NA)
        pl.semaphore_signal(barrier, 1, device_id={"aa": peer}, device_id_type=pl.DeviceIdType.MESH)

    def greet_b(d):
        peer = lax.rem(me_b + d + 1, NB)
        pl.semaphore_signal(barrier, 1, device_id={"ba": peer}, device_id_type=pl.DeviceIdType.MESH)

    loop(NA - 1, greet_a)
    loop(NB - 1, greet_b)

    g1[C] = jnp.zeros((32, NZT), BF)
    g0[C] = jnp.zeros((32, NZT), BF)
    for level in range(2):
        for k in range(3):
            for p in range(2):
                wts[level, k, p, C] = jnp.zeros((C, 432), BF)
    q[256:296] = jnp.zeros((40, 128), F32)
    mm[...] = jnp.zeros(mm.shape, F32)
    mt[...] = jnp.zeros(mt.shape, F32)
    mt0[...] = jnp.zeros(mt0.shape, F32)
    weff[...] = jnp.zeros(weff.shape, F32)
    fold[...] = jnp.zeros(fold.shape, F32)
    sm[...] = jnp.zeros(sm.shape, F32)

    def send(axis, size, src, dst, slot):
        me = me_a if axis == "aa" else me_b

        def one(d):
            peer = lax.rem(me + d + 1, size)
            pltpu.make_async_remote_copy(
                src_ref=src.at[peer],
                dst_ref=dst.at[me],
                send_sem=send_sem.at[slot],
                recv_sem=recv_sem.at[slot],
                device_id={axis: peer},
                device_id_type=pl.DeviceIdType.MESH,
            ).start()

        loop(size - 1, one)
        dst[me] = src[me]

    def arrive(size, dst, slot):
        part = dst.at[pl.ds(0, size - 1)]
        pltpu.make_async_copy(part, part, recv_sem.at[slot]).wait()

    def drain(size, src, slot):
        part = src.at[pl.ds(0, size - 1)]
        pltpu.make_async_copy(part, part, send_sem.at[slot]).wait()

    def pack(g, dst):
        for a in range(NA):
            t, j = a // 3, a % 3
            for half in range(2):
                low = high = None
                for c in range(GC):
                    piece = tbuf[32 * c + 16 * half : 32 * c + 16 * half + 16, 128 * t : 128 * t + 128]
                    shift = (LM * c - LM * j) % 128
                    if shift:
                        piece = pltpu.roll(piece, shift, 1)
                    start = LM * c
                    if start < 128:
                        low = piece if low is None else jnp.where(lanes(16) < start, low, piece)
                    if start + LM > 128:
                        high = piece if high is None else jnp.where(lanes(16) < start - 128, high, piece)
                dst[g, a, 16 * half : 16 * half + 16, 0:128] = low.astype(BF)
                dst[g, a, 16 * half : 16 * half + 16, 128:256] = high.astype(BF)

    def forward_zt(field, g):
        tbuf[...] = dot(field[pl.ds(GC * g, GC)].reshape(GC * 32, NZT), plane[...])

    def forward_x(src, dst, g):
        values = src[g].reshape(512, 256)
        out = dot(xf[0], values) + swap(dot(xf[1], values))
        dst[g] = out.astype(BF).reshape(NB, 32, 256)

    def forward_y(src, g):
        values = src[g].reshape(256, 256)
        out = dot(yf_ref[0], values) + swap(dot(yf_ref[1], values))
        full = jnp.concatenate([out, jnp.zeros((48, 256), F32)], 0)
        q[0:256] = full.T
        for p in range(2):
            tiles = [[None] * 4 for _ in range(3)]
            for m in range(18):
                rows = q[pl.ds(2 * m + p, 8, stride=LM), :]
                t, off = divmod(24 * m, 128)
                for k in range(3):
                    shift = (24 * m - 24 * k) % 128
                    piece = pltpu.roll(rows, shift, 1) if shift else rows
                    old = tiles[k][t]
                    tiles[k][t] = piece if old is None else jnp.where(lane < off, old, piece)
                    if off + 24 > 128:
                        tiles[k][t + 1] = piece
            for k in range(3):
                for t in range(4):
                    sm[k, p, g, :, 128 * t : 128 * t + 128] = tiles[k][t]

    def mix(g):
        def one(k):
            for t in range(4):
                size = 128 if t < 3 else 48
                part = slice(128 * t, 128 * t + size)
                re = mm[k, 0, 0:C, part]
                im = mm[k, 1, 0:C, part]
                all_re = sm[k, 0, g, :, part]
                all_im = sm[k, 1, g, :, part]
                for c in range(GC):
                    w_re = wts[1, k, 0, GC * g + c, :, part].astype(F32)
                    w_im = wts[1, k, 1, GC * g + c, :, part].astype(F32)
                    s_re = all_re[c : c + 1]
                    s_im = all_im[c : c + 1]
                    re = re + w_re * s_re + w_im * s_im
                    im = im + w_re * s_im - w_im * s_re
                mm[k, 0, 0:C, part] = re
                mm[k, 1, 0:C, part] = im

        loop(3, one)

    def tile_of(load, m):
        t, off = divmod(24 * m, 128)
        value = load(t)
        if off + 24 > 128:
            value = jnp.where(lane < 64, load(t + 1), value)
        return value

    def back_y(dst, g):
        for m in range(18):
            for p in range(2):
                parts = []
                for k in range(3):
                    value = tile_of(lambda t: mg[g, k, p, :, 128 * t : 128 * t + 128], m)
                    shift = (24 * k - 24 * m) % 128
                    parts.append(pltpu.roll(value, shift, 1) if shift else value)
                row = jnp.where(lane < 24, parts[0], jnp.where(lane < 48, parts[1], parts[2]))
                mt[pl.ds(2 * m + p, 8, stride=LM), :] = row
        values = mt[0:256].astype(BF)
        out = dot_nt(yb_ref[0], values) - swap(dot_nt(yb_ref[1], values))
        dst[g] = out.astype(BF).reshape(NB, 32, 256)

    def back_x(values, width):
        turned = -swap(values.astype(F32))
        return dot(xb[0], values) + dot(xb[1], turned.astype(BF))

    def unpack(src, g):
        for half in range(2):
            for c in range(GC):
                start = LM * c
                for t in range(6):
                    parts = []
                    for j in range(3 if t < 5 else 1):
                        a = 3 * t + j
                        rows = slice(16 * half, 16 * half + 16)
                        low = start // 128
                        value = src[g, a, rows, 128 * low : 128 * low + 128].astype(F32)
                        if start % 128 + LM > 128:
                            other = src[g, a, rows, 128:256].astype(F32)
                            value = jnp.where(lanes(16) < 64, other, value)
                        shift = (LM * j - start) % 128
                        parts.append(pltpu.roll(value, shift, 1) if shift else value)
                    full = parts[0]
                    for j in range(1, len(parts)):
                        full = jnp.where(lanes(16) < LM * j, full, parts[j])
                    bx[32 * c + 16 * half : 32 * c + 16 * half + 16, 128 * t : 128 * t + 128] = full.astype(BF)

    def grad_top(g):
        def one(i):
            c = GC * g + i
            for pair in range(2):
                for n in range(4):
                    part = slice(512 * n, 512 * n + 512)
                    v = pre[1, c, 2 * pair : 2 * pair + 2, :, part].astype(F32).reshape(16, 512)
                    d = cot[c, 2 * pair : 2 * pair + 2, :, part].astype(F32).reshape(16, 512)
                    g1[c, 16 * pair : 16 * pair + 16, part] = (d * slope_of(v)).astype(BF)

        loop(sizes[g], one)

    for g in range(NG):
        loads[2 * g].wait()
        loads[2 * g + 1].wait()
        grad_top(g)
        if g == 0:
            load_plane.wait()
        forward_zt(g1, g)
        pack(g, s1)
        if g == 0:
            pl.semaphore_wait(barrier, NA + NB - 2)
        send("aa", NA, s1.at[g], r1.at[g], g)

    def spread(rows, groups):
        r = lax.broadcasted_iota(jnp.int32, (rows, groups), 0) // 16
        return (r == lax.broadcasted_iota(jnp.int32, (rows, groups), 1)).astype(BF)

    left = dot_nt(spread(336, C), skip_ref[1]).astype(BF)
    wide = dot_nt(left, spread(320, C))
    same = lax.broadcasted_iota(jnp.int32, (336, 320), 0) % 16 == lax.broadcasted_iota(jnp.int32, (336, 320), 1) % 16
    kron[...] = jnp.where(same, wide, 0.0).astype(BF)

    load_xf.wait()

    def stage_x1(g):
        arrive(NA, r1.at[g], g)
        forward_x(r1, s2, g)
        send("ba", NB, s2.at[g], r2.at[g], 3 + g)

    loop(NG, stage_x1)

    load_pre0.wait()

    def slope_one(c):
        for pair in range(2):
            for n in range(4):
                part = slice(512 * n, 512 * n + 512)
                v = pre[0, c, 2 * pair : 2 * pair + 2, :, part].astype(F32).reshape(16, 512)
                slope0[c, 16 * pair : 16 * pair + 16, part] = slope_of(v)

    loop(C, slope_one)

    load_w1.wait()

    def stage_y1(g):
        arrive(NB, r2.at[g], 3 + g)
        forward_y(r2, g)
        mix(g)

    loop(NG, stage_y1)
    for g in range(NG):
        for k in range(3):
            for p in range(2):
                mg[g, k, p] = mm[k, p, GC * g : GC * g + 8, :]

    def stage_yb(g):
        back_y(s3, g)
        send("ba", NB, s3.at[g], r3.at[g], 6 + g)

    loop(NG, stage_yb)
    load_xb.wait()

    def stage_xb(g):
        arrive(NB, r3.at[g], 6 + g)
        out = back_x(r3[g].reshape(256, 256), 256)
        s4[g] = out.astype(BF).reshape(NA, 32, 256)
        send("aa", NA, s4.at[g], r4.at[g], 9 + g)

    loop(NG, stage_xb)

    load_w0.wait()
    lift_col = lift_ref[...]

    def fold_weights(i):
        k = i // 2
        p = lax.rem(i, 2)

        def inner(g):
            for c in range(GC):
                row = jnp.sum(wts[0, k, p, GC * g + c].astype(F32) * lift_col, 0, keepdims=True)
                weff[k, p, g, c : c + 1, 0:432] = row

        loop(NG, inner)

    loop(6, fold_weights)

    def stage_field(g):
        arrive(NA, r4.at[g], 9 + g)
        unpack(r4, g)

        def piece(n):
            part = pl.ds(pl.multiple_of(512 * n, 512), 512)
            spectral = dot_nt(bx[...], plane[part, :])
            spectral = spectral.reshape(GC, 2, 16, 512)
            for pair in range(2):
                skip = dot(
                    kron[pl.ds(112 * g, 112), :],
                    g1[0:C, 16 * pair : 16 * pair + 16, part].reshape(320, 512),
                ).reshape(GC, 16, 512)
                incoming = skip + spectral[:, pair] * SCALE_ZT
                for c in range(GC):
                    slope = slope0[jnp.minimum(GC * g + c, C - 1), 16 * pair : 16 * pair + 16, part]
                    g0[GC * g + c, 16 * pair : 16 * pair + 16, part] = (incoming[c] * slope).astype(BF)

        loop(4, piece)
        forward_zt(g0, g)
        pack(g, t1)
        send("aa", NA, t1.at[g], q1.at[g], 12 + g)

    loop(NG, stage_field)

    def stage_x0(g):
        arrive(NA, q1.at[g], 12 + g)
        forward_x(q1, t2, g)
        send("ba", NB, t2.at[g], q2.at[g], 15 + g)

    loop(NG, stage_x0)

    gain = jnp.sum(skip_ref[0].astype(F32) * lift_ref[...].reshape(1, C), 1, keepdims=True)

    def skip_piece(n):
        part = pl.ds(pl.multiple_of(512 * n, 512), 512)
        for pair in range(2):
            rows = slice(16 * pair, 16 * pair + 16)
            total = jnp.zeros((16, 512), F32)
            for c in range(C):
                total = total + g0[c, rows, part].astype(F32) * gain[c : c + 1, :]
            out_ref[rows, part] = total

    loop(4, skip_piece)

    def stage_y0(g):
        arrive(NB, q2.at[g], 15 + g)
        forward_y(q2, g)
        for k in range(3):
            w_re, w_im = weff[k, 0, g], weff[k, 1, g]
            s_re, s_im = sm[k, 0, g], sm[k, 1, g]
            fold[k] += w_re * s_re + w_im * s_im
            fold[3 + k] += w_re * s_im - w_im * s_re

    loop(NG, stage_y0)

    for i in range(6):
        fa[i : i + 1] = jnp.sum(fold[i], 0, keepdims=True)
    fa[6:8] = jnp.zeros((2, 512), F32)
    for m in range(18):
        value = tile_of(lambda t: fa[:, 128 * t : 128 * t + 128], m)
        shift = (-24 * m) % 128
        vv[8 * m : 8 * m + 8] = pltpu.roll(value, shift, 1) if shift else value
    for p in range(2):
        parts = []
        for k in range(3):
            value = vv[pl.ds(3 * p + k, 18, stride=8), :]
            parts.append(pltpu.roll(value, 24 * k, 1) if k else value)
        full = jnp.where(lanes(18) < 24, parts[0], jnp.where(lanes(18) < 48, parts[1], parts[2]))
        mt0[pl.ds(p, 18, stride=2), :] = full
    values = mt0[...].astype(BF)
    out = dot_nt(yb_ref[0], values) - swap(dot_nt(yb_ref[1], values))
    t3[...] = out.astype(BF).reshape(NB, 32, 128)
    send("ba", NB, t3, q3, 18)
    arrive(NB, q3, 18)
    t4[...] = back_x(q3[...].reshape(256, 128), 128).astype(BF).reshape(NA, 32, 128)
    send("aa", NA, t4, q4, 19)
    arrive(NA, q4, 19)
    for t in range(6):
        full = None
        for j in range(3 if t < 5 else 1):
            value = q4[3 * t + j].astype(F32)
            if j:
                value = jnp.where(lanes(32) < LM * j, full, pltpu.roll(value, LM * j, 1))
            full = value
        bx0[:, 128 * t : 128 * t + 128] = full.astype(BF)

    def last(n):
        part = pl.ds(pl.multiple_of(512 * n, 512), 512)
        out_ref[:, part] += dot_nt(bx0[...], plane[part, :]) * SCALE_ZT

    loop(4, last)

    for g in range(NG):
        drain(NA, s1.at[g], g)
        drain(NB, s2.at[g], 3 + g)
        drain(NB, s3.at[g], 6 + g)
        drain(NA, s4.at[g], 9 + g)
        drain(NA, t1.at[g], 12 + g)
        drain(NB, t2.at[g], 15 + g)
    drain(NB, t3, 18)
    drain(NA, t4, 19)


def per_device(cotangent, pre_activations, spectral_weights, skip_weights, lift_weights):
    bf = lambda table: jnp.asarray(table.astype(np.float32), dtype=BF)
    forward_x_table = x_table()
    back_x_table = forward_x_table.transpose(0, 2, 1) / 64
    any_spec = pl.BlockSpec(memory_space=pl.ANY)
    vmem_spec = pl.BlockSpec(memory_space=pltpu.VMEM)
    block_a, block_b = (NG, NA, 32, 256), (NG, NB, 32, 256)
    scratch = [
        pltpu.VMEM((C, 4, 8, NZT), BF),
        pltpu.VMEM((2, C, 4, 8, NZT), BF),
        pltpu.VMEM((2, 3, 2, C + 1, C, 432), BF),
        pltpu.VMEM((NZT, 768), BF),
        pltpu.VMEM((2, 256, 512), BF),
        pltpu.VMEM((2, 512, 256), BF),
        pltpu.VMEM((C + 1, 32, NZT), BF),
        pltpu.VMEM((C + 1, 32, NZT), BF),
        pltpu.VMEM((C, 32, NZT), F32),
        pltpu.VMEM((224, 768), F32),
        pltpu.VMEM((224, 768), BF),
        pltpu.VMEM((336, 320), BF),
        pltpu.VMEM(block_a, BF), pltpu.VMEM(block_a, BF),
        pltpu.VMEM(block_b, BF), pltpu.VMEM(block_b, BF),
        pltpu.VMEM(block_b, BF), pltpu.VMEM(block_b, BF),
        pltpu.VMEM(block_a, BF), pltpu.VMEM(block_a, BF),
        pltpu.VMEM(block_a, BF), pltpu.VMEM(block_a, BF),
        pltpu.VMEM(block_b, BF), pltpu.VMEM(block_b, BF),
        pltpu.VMEM((NB, 32, 128), BF), pltpu.VMEM((NB, 32, 128), BF),
        pltpu.VMEM((NA, 32, 128), BF), pltpu.VMEM((NA, 32, 128), BF),
        pltpu.VMEM((296, 128), F32),
        pltpu.VMEM((3, 2, NG, 8, 512), F32),
        pltpu.VMEM((3, 2, 24, 512), F32),
        pltpu.VMEM((NG, 3, 2, 8, 512), F32),
        pltpu.VMEM((296, 128), F32),
        pltpu.VMEM((3, 2, NG, 8, 512), F32),
        pltpu.VMEM((6, 8, 512), F32),
        pltpu.VMEM((8, 512), F32),
        pltpu.VMEM((144, 128), F32),
        pltpu.VMEM((128, 128), F32),
        pltpu.VMEM((32, 768), BF),
        pltpu.SemaphoreType.DMA((12,)),
        pltpu.SemaphoreType.DMA((20,)),
        pltpu.SemaphoreType.DMA((20,)),
    ]
    out = pl.pallas_call(
        kernel,
        out_shape=jax.ShapeDtypeStruct((32, NZT), F32),
        in_specs=[any_spec] * 3 + [vmem_spec] * 2 + [any_spec] * 3 + [vmem_spec] * 2,
        out_specs=vmem_spec,
        scratch_shapes=scratch,
        compiler_params=pltpu.CompilerParams(
            collective_id=0, has_side_effects=True, vmem_limit_bytes=64000000
        ),
        name="fno_grad",
    )(
        cotangent.reshape(C, 4, 8, NZT),
        pre_activations.reshape(2, C, 4, 8, NZT),
        spectral_weights.transpose(0, 4, 1, 2, 3, 5),
        skip_weights,
        lift_weights.reshape(C, 1),
        bf(plane_table()),
        bf(forward_x_table),
        bf(back_x_table),
        bf(y_table()),
        bf(y_back_table()),
    )
    return out.reshape(1, 4, 8, NZT)


def solution(mesh):
    return jax.shard_map(
        per_device,
        mesh=mesh,
        in_specs=(
            P(None, None, "aa", "ba", None),
            P(None, None, None, "aa", "ba", None),
            P(None, None, None, None, "ba", "aa"),
            P(),
            P(),
        ),
        out_specs=P(None, "aa", "ba", None),
        check_vma=False,
    )
```

profile of v0, /device:TPU:1, one launch (start us, length us, event | category | flops | bytes accessed | tf_op | source)
XLA Modules:
  0.0 88.1 jit_solution(18404350762927328385)
XLA Ops:
  0.0 1.3 %copy.12.skip_ref = bf16[2,20,20]{2,1,0:T(8,128)(2,1)} copy(bf16[2,20,20]{2,0,1:T(2,128)(2,1)} %param.13) | data formatting | bytes 3200 | tf_op args[3]
  1.3 1.3 %copy.13.lift_ref = f32[20,1]{1,0:T(8,128)} copy(f32[20,1]{0,1:T(1,128)} %bitcast.11) | data formatting | bytes 160 | tf_op jit(solution)/shard_map/reshape | solution.py:562
  2.6 6.0 %copy.15 = bf16[2,2,20,20,3,432]{5,3,2,1,4,0:T(8,128)(2,1)} copy(bf16[2,2,20,20,3,432]{5,1,4,3,2,0:T(2,128)(2,1)} %param.12) | data formatting | bytes 8294400 | tf_op args[2]
  8.6 77.7 %fno_grad.1 = f32[32,2048]{1,0:T(8,128)} custom-call(bf16[20,4,8,2048]{3,2,1,0:T(8,128)(2,1)} %bitcast.9, bf16[2,20,4,8,2048]{4,3,2,1,0:T(8,128)(2,1)} %bitcast.8, bf16[2,3,2,20,20,432]{5,4,3,2,1,0:T(8,128)(2,1)} %bitcast.7, bf16[2,20,20]{2,1,0:T(8,128)(2,1)} %copy.12.skip_ref, f32[20,1]{1,0:T(8,128)} %copy.13.lift_ref, ...), custom_call_target="tpu_custom_call" | custom-call | tf_op jit(solution)/shard_map/fno_grad/pallas_call | solution.py:547
  86.4 1.7 %copy.17 = f32[1,4,8,2048]{3,2,1,0:T(8,128)} copy(f32[1,4,8,2048]{3,2,1,0:T(8,128)} %bitcast.10) | data formatting | bytes 524288
where the time goes:
time: 88.3 us; the launch traced here: 88.1 us
  Pallas kernels  77.7 us (88%)
  local copies, waits for them, and re-layouts  10.3 us (12%)
    pallas_call x1, Pallas kernels, per_device(): pl.pallas_call(kernel, out_shape=jax.ShapeDtypeStruct((32, NZT), F32), in...  77.7 us
    unnamed x3, local copies, waits for them, and re-layouts  8.96 us

commit v1 on v0

--- a/solution.py
+++ b/solution.py
@@ -98,8 +98,8 @@
 
 
 def kernel(
-    cot_h, pre_h, wts_h, skip_ref, lift_ref, plane_h, xf_h, xb_h, yf_ref, yb_ref, out_ref,
-    cot, pre, wts, plane, xf, xb, g1, g0, slope0, tbuf, bx, kron,
+    cot_h, pre_h, wts_h, skip_ref, lift_s, lift_ref, plane_h, xf_h, xb_h, yf_ref, yb_ref, out_ref,
+    cot, pre, wts, plane, xf, xb, g1, g0, slope0, skip1, tbuf, bx, kron, wide,
     s1, r1, s2, r2, s3, r3, s4, r4, t1, q1, t2, q2, t3, q3, t4, q4,
     q, sm, mm, mg, mt, weff, fold, fa, vv, mt0, bx0,
     in_sem, send_sem, recv_sem,
@@ -121,18 +121,11 @@
     load_pre0 = pltpu.make_async_copy(pre_h.at[0], pre.at[0], in_sem.at[7])
     load_xf = pltpu.make_async_copy(xf_h, xf, in_sem.at[8])
     load_xb = pltpu.make_async_copy(xb_h, xb, in_sem.at[9])
-    load_w1 = pltpu.make_async_copy(wts_h.at[1], wts.at[1, :, :, pl.ds(0, C)], in_sem.at[10])
-    load_w0 = pltpu.make_async_copy(wts_h.at[0], wts.at[0, :, :, pl.ds(0, C)], in_sem.at[11])
+    load_w1 = pltpu.make_async_copy(wts_h.at[1], wts.at[1], in_sem.at[10])
+    load_w0 = pltpu.make_async_copy(wts_h.at[0], wts.at[0], in_sem.at[11])
     loads[0].start()
     loads[1].start()
     load_plane.start()
-    for copy in loads[2:]:
-        copy.start()
-    load_xf.start()
-    load_pre0.start()
-    load_w1.start()
-    load_xb.start()
-    load_w0.start()
 
     barrier = pltpu.get_barrier_semaphore()
 
@@ -149,10 +142,10 @@
 
     g1[C] = jnp.zeros((32, NZT), BF)
     g0[C] = jnp.zeros((32, NZT), BF)
-    for level in range(2):
-        for k in range(3):
-            for p in range(2):
-                wts[level, k, p, C] = jnp.zeros((C, 432), BF)
+    for k in range(3):
+        wide[C, k] = jnp.zeros((40, 432), F32)
+    for box in (r2, r3, q2, q3):
+        box[..., 24:32, :] = jnp.zeros(box.shape[:-2] + (8, box.shape[-1]), BF)
     q[256:296] = jnp.zeros((40, 128), F32)
     mm[...] = jnp.zeros(mm.shape, F32)
     mt[...] = jnp.zeros(mt.shape, F32)
@@ -161,29 +154,46 @@
     fold[...] = jnp.zeros(fold.shape, F32)
     sm[...] = jnp.zeros(sm.shape, F32)
 
-    def send(axis, size, src, dst, slot):
+    def partners(axis):
+        if axis == "aa":
+            order = [
+                (1, 2, 0), (1, 2, 1), (1, 1, 0), (1, 3, 0), (1, 1, 1), (1, 3, 1), (1, 0, 0), (1, 0, 1),
+                (0, 2, 0), (0, 2, 1), (0, 1, 0), (0, 3, 0), (0, 1, 1), (0, 3, 1), (0, 0, 1),
+            ]
+            z, x, core = me_a // 8, lax.rem(me_a // 2, 4), lax.rem(me_a, 2)
+            return [
+                lax.rem(z + dz, 2) * 8 + lax.rem(x + dx, 4) * 2 + lax.rem(core + dc, 2)
+                for dz, dx, dc in order
+            ]
+        z, y = me_b // 4, lax.rem(me_b, 4)
+        order = [(1, 2), (0, 2), (1, 1), (1, 3), (0, 1), (0, 3), (1, 0)]
+        return [lax.rem(z + dz, 2) * 4 + lax.rem(y + dy, 4) for dz, dy in order]
+
+    def send(axis, src, dst, slot):
         me = me_a if axis == "aa" else me_b
-
-        def one(d):
-            peer = lax.rem(me + d + 1, size)
+        rows = pl.ds(0, 32 if axis == "aa" else 24)
+        for peer in partners(axis):
             pltpu.make_async_remote_copy(
-                src_ref=src.at[peer],
-                dst_ref=dst.at[me],
+                src_ref=src.at[peer, rows],
+                dst_ref=dst.at[me, rows],
                 send_sem=send_sem.at[slot],
                 recv_sem=recv_sem.at[slot],
                 device_id={axis: peer},
                 device_id_type=pl.DeviceIdType.MESH,
             ).start()
-
-        loop(size - 1, one)
         dst[me] = src[me]
 
-    def arrive(size, dst, slot):
-        part = dst.at[pl.ds(0, size - 1)]
+    def span(axis, box):
+        if axis == "aa":
+            return box.at[pl.ds(0, NA - 1)]
+        return box.at[pl.ds(0, NB - 1), pl.ds(0, 24)]
+
+    def arrive(axis, dst, slot):
+        part = span(axis, dst)
         pltpu.make_async_copy(part, part, recv_sem.at[slot]).wait()
 
-    def drain(size, src, slot):
-        part = src.at[pl.ds(0, size - 1)]
+    def drain(axis, src, slot):
+        part = span(axis, src)
         pltpu.make_async_copy(part, part, send_sem.at[slot]).wait()
 
     def pack(g, dst):
@@ -238,21 +248,26 @@
             for t in range(4):
                 size = 128 if t < 3 else 48
                 part = slice(128 * t, 128 * t + size)
-                re = mm[k, 0, 0:C, part]
-                im = mm[k, 1, 0:C, part]
+                by_re = mm[k, 0, t, 0:40, 0:size]
+                by_im = mm[k, 1, t, 0:40, 0:size]
                 all_re = sm[k, 0, g, :, part]
                 all_im = sm[k, 1, g, :, part]
                 for c in range(GC):
-                    w_re = wts[1, k, 0, GC * g + c, :, part].astype(F32)
-                    w_im = wts[1, k, 1, GC * g + c, :, part].astype(F32)
-                    s_re = all_re[c : c + 1]
-                    s_im = all_im[c : c + 1]
-                    re = re + w_re * s_re + w_im * s_im
-                    im = im + w_re * s_im - w_im * s_re
-                mm[k, 0, 0:C, part] = re
-                mm[k, 1, 0:C, part] = im
+                    w = wide[GC * g + c, k, :, part]
+                    by_re = by_re + w * all_re[c : c + 1]
+                    by_im = by_im + w * all_im[c : c + 1]
+                mm[k, 0, t, 0:40, 0:size] = by_re
+                mm[k, 1, t, 0:40, 0:size] = by_im
 
         loop(3, one)
+
+    def unmix(g):
+        first, second = pl.ds(2 * GC * g, 8, stride=2), pl.ds(2 * GC * g + 1, 8, stride=2)
+        for k in range(3):
+            for t in range(4):
+                part = slice(128 * t, 128 * t + 128)
+                mg[g, k, 0, :, part] = mm[k, 0, t, first, :] + mm[k, 1, t, second, :]
+                mg[g, k, 1, :, part] = mm[k, 1, t, first, :] - mm[k, 0, t, second, :]
 
     def tile_of(load, m):
         t, off = divmod(24 * m, 128)
@@ -318,29 +333,96 @@
         grad_top(g)
         if g == 0:
             load_plane.wait()
+            for copy in loads[2:] + [load_w1, load_xf, load_pre0, load_xb, load_w0]:
+                copy.start()
         forward_zt(g1, g)
         pack(g, s1)
         if g == 0:
             pl.semaphore_wait(barrier, NA + NB - 2)
-        send("aa", NA, s1.at[g], r1.at[g], g)
+        send("aa", s1.at[g], r1.at[g], g)
 
     def spread(rows, groups):
         r = lax.broadcasted_iota(jnp.int32, (rows, groups), 0) // 16
         return (r == lax.broadcasted_iota(jnp.int32, (rows, groups), 1)).astype(BF)
 
-    left = dot_nt(spread(336, C), skip_ref[1]).astype(BF)
-    wide = dot_nt(left, spread(320, C))
-    same = lax.broadcasted_iota(jnp.int32, (336, 320), 0) % 16 == lax.broadcasted_iota(jnp.int32, (336, 320), 1) % 16
-    kron[...] = jnp.where(same, wide, 0.0).astype(BF)
-
+    skip_all = skip_ref[...].astype(F32)
+    left = dot_nt(spread(320, C), skip_all[:, 1, :].astype(BF)).astype(BF)
+    whole = dot_nt(left, spread(320, C))
+    same = lax.broadcasted_iota(jnp.int32, (320, 320), 0) % 16 == lax.broadcasted_iota(jnp.int32, (320, 320), 1) % 16
+    kron[...] = jnp.where(same, whole, 0.0).astype(BF)
+
+    load_w1.wait()
+
+    def widen(o):
+        for k in range(3):
+            for t in range(4):
+                part = slice(128 * t, min(128 * t + 128, 432))
+                wide[o, k, :, part] = wts[1, o, :, k, :, part].reshape(40, part.stop - part.start).astype(F32)
+
+    loop(C, widen)
     load_xf.wait()
 
     def stage_x1(g):
-        arrive(NA, r1.at[g], g)
+        arrive("aa", r1.at[g], g)
         forward_x(r1, s2, g)
-        send("ba", NB, s2.at[g], r2.at[g], 3 + g)
-
-    loop(NG, stage_x1)
+        send("ba", s2.at[g], r2.at[g], 3 + g)
+
+    stage_x1(0)
+
+    def skip_piece1(n):
+        part = pl.ds(pl.multiple_of(512 * n, 512), 512)
+        for pair in range(2):
+            rows = slice(16 * pair, 16 * pair + 16)
+            out = dot(kron[...], g1[0:C, rows, part].reshape(320, 512))
+            skip1[:, rows, part] = out.reshape(C, 16, 512)
+
+    loop(4, skip_piece1)
+    stage_x1(1)
+    stage_x1(2)
+
+    def stage_y1(g):
+        arrive("ba", r2.at[g], 3 + g)
+        forward_y(r2, g)
+        mix(g)
+
+    loop(NG, stage_y1)
+    for g in range(NG):
+        unmix(g)
+
+    def stage_yb(g):
+        back_y(s3, g)
+        send("ba", s3.at[g], r3.at[g], 6 + g)
+
+    loop(NG, stage_yb)
+    load_w0.wait()
+
+    def fold_weights(i):
+        k = i // NG
+        g = lax.rem(i, NG)
+        for c in range(GC):
+            o = jnp.minimum(GC * g + c, C - 1)
+            for t in range(4):
+                part = slice(128 * t, min(128 * t + 128, 432))
+                total = wts[0, o, 0, k, :, part].astype(F32) * lift_s[0]
+                for i in range(1, C):
+                    total = total + wts[0, o, i, k, :, part].astype(F32) * lift_s[i]
+                weff[k, 0, g, c : c + 1, part] = total[0:1]
+                weff[k, 1, g, c : c + 1, part] = total[1:2]
+
+    loop(9, fold_weights)
+    for k in range(3):
+        for p in range(2):
+            weff[k, p, 2, 6:7] = jnp.zeros((1, 512), F32)
+
+    load_xb.wait()
+
+    def stage_xb(g):
+        arrive("ba", r3.at[g], 6 + g)
+        out = back_x(r3[g].reshape(256, 256), 256)
+        s4[g] = out.astype(BF).reshape(NA, 32, 256)
+        send("aa", s4.at[g], r4.at[g], 9 + g)
+
+    loop(NG, stage_xb)
 
     load_pre0.wait()
 
@@ -353,52 +435,8 @@
 
     loop(C, slope_one)
 
-    load_w1.wait()
-
-    def stage_y1(g):
-        arrive(NB, r2.at[g], 3 + g)
-        forward_y(r2, g)
-        mix(g)
-
-    loop(NG, stage_y1)
-    for g in range(NG):
-        for k in range(3):
-            for p in range(2):
-                mg[g, k, p] = mm[k, p, GC * g : GC * g + 8, :]
-
-    def stage_yb(g):
-        back_y(s3, g)
-        send("ba", NB, s3.at[g], r3.at[g], 6 + g)
-
-    loop(NG, stage_yb)
-    load_xb.wait()
-
-    def stage_xb(g):
-        arrive(NB, r3.at[g], 6 + g)
-        out = back_x(r3[g].reshape(256, 256), 256)
-        s4[g] = out.astype(BF).reshape(NA, 32, 256)
-        send("aa", NA, s4.at[g], r4.at[g], 9 + g)
-
-    loop(NG, stage_xb)
-
-    load_w0.wait()
-    lift_col = lift_ref[...]
-
-    def fold_weights(i):
-        k = i // 2
-        p = lax.rem(i, 2)
-
-        def inner(g):
-            for c in range(GC):
-                row = jnp.sum(wts[0, k, p, GC * g + c].astype(F32) * lift_col, 0, keepdims=True)
-                weff[k, p, g, c : c + 1, 0:432] = row
-
-        loop(NG, inner)
-
-    loop(6, fold_weights)
-
     def stage_field(g):
-        arrive(NA, r4.at[g], 9 + g)
+        arrive("aa", r4.at[g], 9 + g)
         unpack(r4, g)
 
         def piece(n):
@@ -406,30 +444,27 @@
             spectral = dot_nt(bx[...], plane[part, :])
             spectral = spectral.reshape(GC, 2, 16, 512)
             for pair in range(2):
-                skip = dot(
-                    kron[pl.ds(112 * g, 112), :],
-                    g1[0:C, 16 * pair : 16 * pair + 16, part].reshape(320, 512),
-                ).reshape(GC, 16, 512)
-                incoming = skip + spectral[:, pair] * SCALE_ZT
+                rows = slice(16 * pair, 16 * pair + 16)
                 for c in range(GC):
-                    slope = slope0[jnp.minimum(GC * g + c, C - 1), 16 * pair : 16 * pair + 16, part]
-                    g0[GC * g + c, 16 * pair : 16 * pair + 16, part] = (incoming[c] * slope).astype(BF)
+                    o = jnp.minimum(GC * g + c, C - 1)
+                    incoming = skip1[o, rows, part] + spectral[c, pair] * SCALE_ZT
+                    g0[GC * g + c, rows, part] = (incoming * slope0[o, rows, part]).astype(BF)
 
         loop(4, piece)
         forward_zt(g0, g)
         pack(g, t1)
-        send("aa", NA, t1.at[g], q1.at[g], 12 + g)
+        send("aa", t1.at[g], q1.at[g], 12 + g)
 
     loop(NG, stage_field)
 
     def stage_x0(g):
-        arrive(NA, q1.at[g], 12 + g)
+        arrive("aa", q1.at[g], 12 + g)
         forward_x(q1, t2, g)
-        send("ba", NB, t2.at[g], q2.at[g], 15 + g)
+        send("ba", t2.at[g], q2.at[g], 15 + g)
 
     loop(NG, stage_x0)
 
-    gain = jnp.sum(skip_ref[0].astype(F32) * lift_ref[...].reshape(1, C), 1, keepdims=True)
+    gain = jnp.sum(skip_all[:, 0, :] * lift_ref[...], 1, keepdims=True)
 
     def skip_piece(n):
         part = pl.ds(pl.multiple_of(512 * n, 512), 512)
@@ -443,7 +478,7 @@
     loop(4, skip_piece)
 
     def stage_y0(g):
-        arrive(NB, q2.at[g], 15 + g)
+        arrive("ba", q2.at[g], 15 + g)
         forward_y(q2, g)
         for k in range(3):
             w_re, w_im = weff[k, 0, g], weff[k, 1, g]
@@ -470,11 +505,11 @@
     values = mt0[...].astype(BF)
     out = dot_nt(yb_ref[0], values) - swap(dot_nt(yb_ref[1], values))
     t3[...] = out.astype(BF).reshape(NB, 32, 128)
-    send("ba", NB, t3, q3, 18)
-    arrive(NB, q3, 18)
+    send("ba", t3, q3, 18)
+    arrive("ba", q3, 18)
     t4[...] = back_x(q3[...].reshape(256, 128), 128).astype(BF).reshape(NA, 32, 128)
-    send("aa", NA, t4, q4, 19)
-    arrive(NA, q4, 19)
+    send("aa", t4, q4, 19)
+    arrive("aa", q4, 19)
     for t in range(6):
         full = None
         for j in range(3 if t < 5 else 1):
@@ -491,14 +526,14 @@
     loop(4, last)
 
     for g in range(NG):
-        drain(NA, s1.at[g], g)
-        drain(NB, s2.at[g], 3 + g)
-        drain(NB, s3.at[g], 6 + g)
-        drain(NA, s4.at[g], 9 + g)
-        drain(NA, t1.at[g], 12 + g)
-        drain(NB, t2.at[g], 15 + g)
-    drain(NB, t3, 18)
-    drain(NA, t4, 19)
+        drain("aa", s1.at[g], g)
+        drain("ba", s2.at[g], 3 + g)
+        drain("ba", s3.at[g], 6 + g)
+        drain("aa", s4.at[g], 9 + g)
+        drain("aa", t1.at[g], 12 + g)
+        drain("ba", t2.at[g], 15 + g)
+    drain("ba", t3, 18)
+    drain("aa", t4, 19)
 
 
 def per_device(cotangent, pre_activations, spectral_weights, skip_weights, lift_weights):
@@ -507,20 +542,23 @@
     back_x_table = forward_x_table.transpose(0, 2, 1) / 64
     any_spec = pl.BlockSpec(memory_space=pl.ANY)
     vmem_spec = pl.BlockSpec(memory_space=pltpu.VMEM)
+    smem_spec = pl.BlockSpec(memory_space=pltpu.SMEM)
     block_a, block_b = (NG, NA, 32, 256), (NG, NB, 32, 256)
     scratch = [
         pltpu.VMEM((C, 4, 8, NZT), BF),
         pltpu.VMEM((2, C, 4, 8, NZT), BF),
-        pltpu.VMEM((2, 3, 2, C + 1, C, 432), BF),
+        pltpu.VMEM((2, C, C, 3, 2, 432), BF),
         pltpu.VMEM((NZT, 768), BF),
         pltpu.VMEM((2, 256, 512), BF),
         pltpu.VMEM((2, 512, 256), BF),
         pltpu.VMEM((C + 1, 32, NZT), BF),
         pltpu.VMEM((C + 1, 32, NZT), BF),
         pltpu.VMEM((C, 32, NZT), F32),
+        pltpu.VMEM((C, 32, NZT), F32),
         pltpu.VMEM((224, 768), F32),
         pltpu.VMEM((224, 768), BF),
-        pltpu.VMEM((336, 320), BF),
+        pltpu.VMEM((320, 320), BF),
+        pltpu.VMEM((C + 1, 3, 40, 432), F32),
         pltpu.VMEM(block_a, BF), pltpu.VMEM(block_a, BF),
         pltpu.VMEM(block_b, BF), pltpu.VMEM(block_b, BF),
         pltpu.VMEM(block_b, BF), pltpu.VMEM(block_b, BF),
@@ -531,7 +569,7 @@
         pltpu.VMEM((NA, 32, 128), BF), pltpu.VMEM((NA, 32, 128), BF),
         pltpu.VMEM((296, 128), F32),
         pltpu.VMEM((3, 2, NG, 8, 512), F32),
-        pltpu.VMEM((3, 2, 24, 512), F32),
+        pltpu.VMEM((3, 2, 4, 48, 128), F32),
         pltpu.VMEM((NG, 3, 2, 8, 512), F32),
         pltpu.VMEM((296, 128), F32),
         pltpu.VMEM((3, 2, NG, 8, 512), F32),
@@ -547,7 +585,7 @@
     out = pl.pallas_call(
         kernel,
         out_shape=jax.ShapeDtypeStruct((32, NZT), F32),
-        in_specs=[any_spec] * 3 + [vmem_spec] * 2 + [any_spec] * 3 + [vmem_spec] * 2,
+        in_specs=[any_spec] * 3 + [vmem_spec, smem_spec, vmem_spec] + [any_spec] * 3 + [vmem_spec] * 2,
         out_specs=vmem_spec,
         scratch_shapes=scratch,
         compiler_params=pltpu.CompilerParams(
@@ -557,9 +595,10 @@
     )(
         cotangent.reshape(C, 4, 8, NZT),
         pre_activations.reshape(2, C, 4, 8, NZT),
-        spectral_weights.transpose(0, 4, 1, 2, 3, 5),
-        skip_weights,
-        lift_weights.reshape(C, 1),
+        spectral_weights.transpose(0, 2, 3, 4, 1, 5),
+        skip_weights.transpose(1, 0, 2),
+        lift_weights,
+        lift_weights.reshape(1, C),
         bf(plane_table()),
         bf(forward_x_table),
         bf(back_x_table),

time: 88.3 us -> 73.7 us (0.83)
  local copies, waits for them, and re-layouts: 10.3 us -> 1.67 us
  Pallas kernels: 77.7 us -> 71.9 us
    unnamed x3 -> x1, local copies, waits for them, and re-layouts: 8.96 us -> 1.67 us
    pallas_call x1, Pallas kernels: 77.7 us -> 71.9 us  [per_device(): pl.pallas_call(kernel, out_shape=jax.ShapeDtypeStruct((32, NZT), F32), in...]
    reshape x1 -> x0, local copies, waits for them, and re-layouts: 1.33 us -> none  [per_device(): lift_weights.reshape(C, 1)]
where the time goes in v1:
time: 73.7 us; the launch traced here: 73.6 us
  Pallas kernels  71.9 us (98%)
  local copies, waits for them, and re-layouts  1.67 us (2%)
    pallas_call x1, Pallas kernels, per_device(): pl.pallas_call(kernel, out_shape=jax.ShapeDtypeStruct((32, NZT), F32), in...  71.9 us
    unnamed x1, local copies, waits for them, and re-layouts  1.67 us

profile of v1, /device:TPU:1, one launch (start us, length us, event | category | flops | bytes accessed | tf_op | source)
XLA Modules:
  0.0 73.6 jit_solution(15241624445326710616)
XLA Ops:
  0.0 71.9 %fno_grad.1 = f32[32,2048]{1,0:T(8,128)} custom-call(bf16[20,4,8,2048]{3,2,1,0:T(8,128)(2,1)} %bitcast.8, bf16[2,20,4,8,2048]{4,3,2,1,0:T(8,128)(2,1)} %bitcast.6, bf16[2,20,20,3,2,432]{5,4,3,2,1,0:T(2,128)(2,1)} %bitcast.7, bf16[20,2,20]{2,1,0:T(2,128)(2,1)} %bitcast.10, f32[20]{0:T(128)} %lift_s.1, f32[1,20]{1,0:T(1,128)} %bitcast.11, ...), custom_call_target="tpu_custom_call" | custom-call | tf_op jit(solution)/shard_map/fno_grad/pallas_call | solution.py:585
  71.9 1.7 %copy.12 = f32[1,4,8,2048]{3,2,1,0:T(8,128)} copy(f32[1,4,8,2048]{3,2,1,0:T(8,128)} %bitcast.9) | data formatting | bytes 524288

commit v2 on v1

v2 whole, which is shorter than its diff:
```python
import math

import jax
import jax.numpy as jnp
import numpy as np
from jax import lax
from jax.experimental import pallas as pl
from jax.experimental.pallas import tpu as pltpu
from jax.sharding import PartitionSpec as P

C = 20
NZT = 2048
NA = 16
NB = 8
NG = 4
START = (0, 3, 10, 17)
COUNT = (3, 7, 7, 3)
WIDTH = (128, 256, 256, 128)
LM = 36
SCALE_ZT = 1.0 / NZT
BF = jnp.bfloat16
F32 = jnp.float32
INV_SQRT2 = 1.0 / math.sqrt(2.0)
INV_SQRT2PI = 1.0 / math.sqrt(2.0 * math.pi)


def freq(count):
    j = np.arange(count)
    return np.where(j < count // 2, j, j - count)


def plane_table():
    joint = np.arange(24 * 12)
    kz = freq(24)[joint // 12]
    kt = joint % 12
    cell = np.arange(NZT)
    turns = (kz[None, :] * (cell[:, None] // 32) * 32 + kt[None, :] * (cell[:, None] % 32) * 64) % NZT
    angle = 2.0 * np.pi / NZT * turns
    table = np.zeros((NZT, 768))
    owner, local = joint // 18, joint % 18
    column = 128 * (owner // 3) + LM * (owner % 3) + 2 * local
    table[:, column] = np.cos(angle)
    table[:, column + 1] = -np.sin(angle)
    return table


def line_angle():
    return 2.0 * np.pi / 64 * ((freq(24)[:, None] * np.arange(64)[None, :]) % 64)


def x_table():
    angle = line_angle()
    out = np.zeros((2, NB, 4, 8, 64, 8))
    for y in range(8):
        out[0, :, :3, y, :, y] = np.cos(angle).reshape(NB, 3, 64)
        out[1, :, :3, y, :, y] = np.sin(angle).reshape(NB, 3, 64)
    return out.reshape(2, 256, 512)


def y_table():
    angle = line_angle().reshape(24, NB, 8)
    out = np.zeros((2, 80, NB, 4, 8))
    for k in range(3):
        out[0, 24 * k : 24 * k + 24, :, k] = np.cos(angle)
        out[1, 24 * k : 24 * k + 24, :, k] = np.sin(angle)
    return out.reshape(2, 80, 256)


def y_back_table():
    wide = np.zeros((2, 256, 128))
    wide[:, :, :80] = y_table().transpose(0, 2, 1) / 64
    return wide


def quarter_signs():
    joint = np.arange(24 * 12)
    rest = freq(24)[joint // 12] % 4
    owner, local = joint // 18, joint % 18
    column = 128 * (owner // 3) + LM * (owner % 3) + 2 * local
    table = np.zeros((8, 768))
    for part in range(2):
        table[0, column + part] = rest % 2 == 0
        table[1, column + part] = np.where(rest % 2 == 0, 1 - rest, 0)
        table[2, column + part] = rest % 2
        table[3, column + part] = np.where(rest % 2 == 1, rest - 2, 0)
    return table


def swap(values):
    even = lax.broadcasted_iota(jnp.int32, (values.shape[0], 128), 1) % 2 == 0
    parts = []
    for t in range(values.shape[1] // 128):
        part = values[:, 128 * t : 128 * t + 128]
        parts.append(jnp.where(even, pltpu.roll(part, 127, 1), -pltpu.roll(part, 1, 1)))
    return parts[0] if len(parts) == 1 else jnp.concatenate(parts, 1)


def dot(a, b):
    return jnp.dot(a, b, preferred_element_type=F32)


def dot_nt(a, b):
    return lax.dot_general(a, b, (((1,), (1,)), ((), ())), preferred_element_type=F32)


def slope_of(v):
    normal_cdf = 0.5 + 0.5 * lax.erf(v * INV_SQRT2)
    return normal_cdf + v * (jnp.exp(-0.5 * v * v) * INV_SQRT2PI)


def loop(count, body):
    lax.fori_loop(0, count, lambda i, carry: (body(i), carry)[1], 0)


def kernel(
    cot_h, pre_h, wts_h, skip_h, lift_h, plane_h, xf_h, xb_h, yf_h, yb_h, signs_h, out_ref,
    cot, pre, wts, skip_ref, lift_ref, plane, xf, xb, yf_ref, yb_ref, signs,
    g1, g0, slope0, skip1, bx, kron, wide,
    s1n, r1n, s2n, r2n, s3n, r3n, s4n, r4n, t1n, q1n, t2n, q2n,
    s1w, r1w, s2w, r2w, s3w, r3w, s4w, r4w, t1w, q1w, t2w, q2w,
    t3, q3, t4, q4,
    q, sm, mm, mg, mt, weff, fold, fa, vv, mt0, bx0, lift_rows,
    in_sem, send_sem, recv_sem,
):
    me_a = lax.axis_index("aa")
    me_b = lax.axis_index("ba")
    lane = lax.broadcasted_iota(jnp.int32, (8, 128), 1)
    row8 = lax.broadcasted_iota(jnp.int32, (8, 128), 0)

    def lanes(rows):
        return lax.broadcasted_iota(jnp.int32, (rows, 128), 1)

    def boxes(narrow, wide_box):
        return [narrow.at[0], wide_box.at[0], wide_box.at[1], narrow.at[1]]

    s1, r1, s2, r2 = boxes(s1n, s1w), boxes(r1n, r1w), boxes(s2n, s2w), boxes(r2n, r2w)
    s3, r3, s4, r4 = boxes(s3n, s3w), boxes(r3n, r3w), boxes(s4n, s4w), boxes(r4n, r4w)
    t1, q1, t2, q2 = boxes(t1n, t1w), boxes(q1n, q1w), boxes(t2n, t2w), boxes(q2n, q2w)

    loads = []
    for g in range(NG):
        part = pl.ds(START[g], COUNT[g])
        loads.append(pltpu.make_async_copy(cot_h.at[part], cot.at[part], in_sem.at[2 * g]))
        loads.append(pltpu.make_async_copy(pre_h.at[1, part], pre.at[1, part], in_sem.at[2 * g + 1]))
    load_plane = pltpu.make_async_copy(plane_h, plane, in_sem.at[8])
    load_pre0 = pltpu.make_async_copy(pre_h.at[0], pre.at[0], in_sem.at[9])
    load_xf = pltpu.make_async_copy(xf_h, xf, in_sem.at[10])
    load_xb = pltpu.make_async_copy(xb_h, xb, in_sem.at[11])
    load_w1 = pltpu.make_async_copy(wts_h.at[1], wts.at[1], in_sem.at[12])
    load_w0 = pltpu.make_async_copy(wts_h.at[0], wts.at[0], in_sem.at[13])
    load_yf = pltpu.make_async_copy(yf_h, yf_ref, in_sem.at[14])
    load_yb = pltpu.make_async_copy(yb_h, yb_ref, in_sem.at[15])
    load_skip = pltpu.make_async_copy(skip_h, skip_ref, in_sem.at[16])
    load_lift = pltpu.make_async_copy(lift_h, lift_ref, in_sem.at[17])
    load_signs = pltpu.make_async_copy(signs_h, signs, in_sem.at[18])
    loads[0].start()
    loads[1].start()
    load_plane.start()

    barrier = pltpu.get_barrier_semaphore()

    def greet_a(d):
        peer = lax.rem(me_a + d + 1, NA)
        pl.semaphore_signal(barrier, 1, device_id={"aa": peer}, device_id_type=pl.DeviceIdType.MESH)

    def greet_b(d):
        peer = lax.rem(me_b + d + 1, NB)
        pl.semaphore_signal(barrier, 1, device_id={"ba": peer}, device_id_type=pl.DeviceIdType.MESH)

    loop(NA - 1, greet_a)
    loop(NB - 1, greet_b)

    for box in (r2n, r3n, q2n, r2w, r3w, q2w, q3):
        box[..., 24:32, :] = jnp.zeros(box.shape[:-2] + (8, box.shape[-1]), BF)
    mm[...] = jnp.zeros(mm.shape, F32)
    mt[...] = jnp.zeros(mt.shape, F32)
    mt0[...] = jnp.zeros(mt0.shape, F32)
    weff[...] = jnp.zeros(weff.shape, F32)
    fold[...] = jnp.zeros(fold.shape, F32)
    sm[...] = jnp.zeros(sm.shape, F32)

    def partners(axis):
        if axis == "aa":
            order = [
                (1, 2, 0), (1, 2, 1), (1, 1, 0), (1, 3, 0), (1, 1, 1), (1, 3, 1), (1, 0, 0), (1, 0, 1),
                (0, 2, 0), (0, 2, 1), (0, 1, 0), (0, 3, 0), (0, 1, 1), (0, 3, 1), (0, 0, 1),
            ]
            z, x, core = me_a // 8, lax.rem(me_a // 2, 4), lax.rem(me_a, 2)
            return [
                lax.rem(z + dz, 2) * 8 + lax.rem(x + dx, 4) * 2 + lax.rem(core + dc, 2)
                for dz, dx, dc in order
            ]
        z, y = me_b // 4, lax.rem(me_b, 4)
        order = [(1, 2), (0, 2), (1, 1), (1, 3), (0, 1), (0, 3), (1, 0)]
        return [lax.rem(z + dz, 2) * 4 + lax.rem(y + dy, 4) for dz, dy in order]

    def send(axis, src, dst, slot):
        me = me_a if axis == "aa" else me_b
        rows = pl.ds(0, 32 if axis == "aa" else 24)
        for peer in partners(axis):
            pltpu.make_async_remote_copy(
                src_ref=src.at[peer, rows],
                dst_ref=dst.at[me, rows],
                send_sem=send_sem.at[slot],
                recv_sem=recv_sem.at[slot],
                device_id={axis: peer},
                device_id_type=pl.DeviceIdType.MESH,
            ).start()
        dst[me] = src[me]

    def span(axis, box):
        if axis == "aa":
            return box.at[pl.ds(0, NA - 1)]
        return box.at[pl.ds(0, NB - 1), pl.ds(0, 24)]

    def arrive(axis, dst, slot):
        part = span(axis, dst)
        pltpu.make_async_copy(part, part, recv_sem.at[slot]).wait()

    def drain(axis, src, slot):
        part = span(axis, src)
        pltpu.make_async_copy(part, part, send_sem.at[slot]).wait()

    def forward_zt(field, g, dst):
        values = field[START[g] : START[g] + COUNT[g]].reshape(COUNT[g] * 32, NZT)
        for block in range(3):
            out = dot(values, plane[:, 256 * block : 256 * block + 256])
            for a in range(6 * block, min(6 * block + 6, NA)):
                t, j = a // 3 - 2 * block, a % 3
                low = high = None
                for c in range(COUNT[g]):
                    piece = out[32 * c : 32 * c + 32, 128 * t : 128 * t + 128]
                    shift = (LM * c - LM * j) % 128
                    if shift:
                        piece = pltpu.roll(piece, shift, 1)
                    start = LM * c
                    if start < 128:
                        low = piece if low is None else jnp.where(lanes(32) < start, low, piece)
                    if start + LM > 128:
                        high = piece if high is None else jnp.where(lanes(32) < start - 128, high, piece)
                dst[a, :, 0:128] = low.astype(BF)
                if high is not None:
                    dst[a, :, 128:256] = high.astype(BF)

    def forward_x(src, dst, g):
        values = src[...].reshape(512, WIDTH[g])
        out = dot(xf[0], values) + swap(dot(xf[1], values))
        dst[...] = out.astype(BF).reshape(NB, 32, WIDTH[g])

    def forward_y(src, g):
        size = WIDTH[g]
        values = src[...].reshape(256, size)
        out = dot(yf_ref[0], values) + swap(dot(yf_ref[1], values))
        full = jnp.concatenate([out, jnp.zeros((48, size), F32)], 0)
        q[0:size] = full.T
        for p in range(2):
            tiles = [[None] * 4 for _ in range(3)]
            for m in range(18):
                rows = q[pl.ds(2 * m + p, 8, stride=LM), :]
                rows = jnp.where(row8 < COUNT[g], rows, 0.0)
                t, off = divmod(24 * m, 128)
                for k in range(3):
                    shift = (24 * m - 24 * k) % 128
                    piece = pltpu.roll(rows, shift, 1) if shift else rows
                    old = tiles[k][t]
                    tiles[k][t] = piece if old is None else jnp.where(lane < off, old, piece)
                    if off + 24 > 128:
                        tiles[k][t + 1] = piece
            for k in range(3):
                for t in range(4):
                    sm[k, p, g, :, 128 * t : 128 * t + 128] = tiles[k][t]

    def mix(g):
        def one(k):
            for t in range(4):
                size = 128 if t < 3 else 48
                part = slice(128 * t, 128 * t + size)
                by_re = mm[k, 0, t, 0:40, 0:size]
                by_im = mm[k, 1, t, 0:40, 0:size]
                all_re = sm[k, 0, g, :, part]
                all_im = sm[k, 1, g, :, part]
                for c in range(COUNT[g]):
                    w = wide[START[g] + c, k, :, part]
                    by_re = by_re + w * all_re[c : c + 1]
                    by_im = by_im + w * all_im[c : c + 1]
                mm[k, 0, t, 0:40, 0:size] = by_re
                mm[k, 1, t, 0:40, 0:size] = by_im

        loop(3, one)

    def unmix(g):
        first, second = pl.ds(2 * START[g], 8, stride=2), pl.ds(2 * START[g] + 1, 8, stride=2)
        for k in range(3):
            for t in range(4):
                part = slice(128 * t, 128 * t + 128)
                mg[k, 0, :, part] = mm[k, 0, t, first, :] + mm[k, 1, t, second, :]
                mg[k, 1, :, part] = mm[k, 1, t, first, :] - mm[k, 0, t, second, :]

    def tile_of(load, m):
        t, off = divmod(24 * m, 128)
        value = load(t)
        if off + 24 > 128:
            value = jnp.where(lane < 64, load(t + 1), value)
        return value

    def back_y(dst, g):
        for m in range(18):
            for p in range(2):
                parts = []
                for k in range(3):
                    value = tile_of(lambda t: mg[k, p, :, 128 * t : 128 * t + 128], m)
                    shift = (24 * k - 24 * m) % 128
                    parts.append(pltpu.roll(value, shift, 1) if shift else value)
                row = jnp.where(lane < 24, parts[0], jnp.where(lane < 48, parts[1], parts[2]))
                mt[pl.ds(2 * m + p, 8, stride=LM), :] = row
        values = mt[0 : WIDTH[g]].astype(BF)
        out = dot_nt(yb_ref[0], values) - swap(dot_nt(yb_ref[1], values))
        dst[...] = out.astype(BF).reshape(NB, 32, WIDTH[g])

    def back_x(values):
        turned = -swap(values.astype(F32))
        return dot(xb[0], values) + dot(xb[1], turned.astype(BF))

    def unpack(src, g):
        for c in range(COUNT[g]):
            start = LM * c
            low = start // 128
            for t in range(6):
                full = None
                for j in range(3 if t < 5 else 1):
                    a = 3 * t + j
                    value = src[a, :, 128 * low : 128 * low + 128].astype(F32)
                    if start % 128 + LM > 128:
                        value = jnp.where(lanes(32) < 64, src[a, :, 128:256].astype(F32), value)
                    shift = (LM * j - start) % 128
                    value = pltpu.roll(value, shift, 1) if shift else value
                    full = value if full is None else jnp.where(lanes(32) < LM * j, full, value)
                bx[32 * c : 32 * c + 32, 128 * t : 128 * t + 128] = full.astype(BF)

    def grad_top(g):
        def one(i):
            c = START[g] + i
            for pair in range(2):
                for n in range(4):
                    part = slice(512 * n, 512 * n + 512)
                    v = pre[1, c, 2 * pair : 2 * pair + 2, :, part].astype(F32).reshape(16, 512)
                    d = cot[c, 2 * pair : 2 * pair + 2, :, part].astype(F32).reshape(16, 512)
                    g1[c, 16 * pair : 16 * pair + 16, part] = (d * slope_of(v)).astype(BF)

        loop(COUNT[g], one)

    for g in range(NG):
        loads[2 * g].wait()
        loads[2 * g + 1].wait()
        if g == 0:
            for copy in loads[2:4]:
                copy.start()
        grad_top(g)
        if g == 0:
            load_plane.wait()
            late = [load_skip, load_w1, load_xf, load_yf, load_yb, load_xb, load_lift, load_w0, load_pre0, load_signs]
            for copy in loads[4:] + late:
                copy.start()
        forward_zt(g1, g, s1[g])
        if g == 0:
            pl.semaphore_wait(barrier, NA + NB - 2)
        send("aa", s1[g], r1[g], g)

    def spread(rows, groups):
        r = lax.broadcasted_iota(jnp.int32, (rows, groups), 0) // 16
        return (r == lax.broadcasted_iota(jnp.int32, (rows, groups), 1)).astype(BF)

    load_skip.wait()
    skip_all = skip_ref[...].astype(F32)
    left = dot_nt(spread(320, C), skip_all[:, 1, :].astype(BF)).astype(BF)
    whole = dot_nt(left, spread(320, C))
    same = lax.broadcasted_iota(jnp.int32, (320, 320), 0) % 16 == lax.broadcasted_iota(jnp.int32, (320, 320), 1) % 16
    kron[...] = jnp.where(same, whole, 0.0).astype(BF)
    load_w1.wait()

    def widen(o):
        for k in range(3):
            for t in range(4):
                part = slice(128 * t, min(128 * t + 128, 432))
                wide[o, k, :, part] = wts[1, o, :, k, :, part].reshape(40, part.stop - part.start).astype(F32)

    loop(C, widen)
    load_xf.wait()

    def stage_x1(g):
        arrive("aa", r1[g], g)
        forward_x(r1[g], s2[g], g)
        send("ba", s2[g], r2[g], 4 + g)

    stage_x1(0)

    def skip_piece1(n):
        part = pl.ds(pl.multiple_of(512 * n, 512), 512)
        for pair in range(2):
            rows = slice(16 * pair, 16 * pair + 16)
            out = dot(kron[...], g1[:, rows, part].reshape(320, 512))
            skip1[:, rows, part] = out.reshape(C, 16, 512)

    loop(4, skip_piece1)
    for g in range(1, NG):
        stage_x1(g)

    load_yf.wait()
    for g in range(NG):
        arrive("ba", r2[g], 4 + g)
        forward_y(r2[g], g)
        mix(g)

    load_yb.wait()
    for g in range(NG):
        unmix(g)
        back_y(s3[g], g)
        send("ba", s3[g], r3[g], 8 + g)

    load_lift.wait()
    for i in range(C):
        lift_rows[i] = jnp.broadcast_to(lift_ref[:, i : i + 1], (2, 128))
    load_w0.wait()

    def fold_weights(k):
        for t in range(4):
            part = slice(128 * t, min(128 * t + 128, 432))
            size = part.stop - part.start
            for o in range(C):
                total = wts[0, o, 0, k, :, part].astype(F32) * lift_rows[0, :, 0:size]
                for i in range(1, C):
                    total = total + wts[0, o, i, k, :, part].astype(F32) * lift_rows[i, :, 0:size]
                weff[k, 0, o : o + 1, part] = total[0:1]
                weff[k, 1, o : o + 1, part] = total[1:2]

    loop(3, fold_weights)
    load_xb.wait()
    for g in range(NG):
        arrive("ba", r3[g], 8 + g)
        out = back_x(r3[g][...].reshape(256, WIDTH[g]))
        s4[g][...] = out.astype(BF).reshape(NA, 32, WIDTH[g])
        send("aa", s4[g], r4[g], 12 + g)

    load_pre0.wait()

    def slope_one(c):
        for pair in range(2):
            for n in range(4):
                part = slice(512 * n, 512 * n + 512)
                v = pre[0, c, 2 * pair : 2 * pair + 2, :, part].astype(F32).reshape(16, 512)
                slope0[c, 16 * pair : 16 * pair + 16, part] = slope_of(v)

    loop(C, slope_one)

    for g in range(NG):
        arrive("aa", r4[g], 12 + g)
        unpack(r4[g], g)

        def piece(n):
            part = pl.ds(pl.multiple_of(512 * n, 512), 512)
            spectral = dot_nt(bx[0 : 32 * COUNT[g]], plane[part, :]).reshape(COUNT[g], 32, 512)
            for c in range(COUNT[g]):
                o = START[g] + c
                incoming = skip1[o, :, part] + spectral[c] * SCALE_ZT
                g0[o, :, part] = (incoming * slope0[o, :, part]).astype(BF)

        loop(4, piece)
        forward_zt(g0, g, t1[g])
        send("aa", t1[g], q1[g], 16 + g)

    for g in range(NG):
        arrive("aa", q1[g], 16 + g)
        forward_x(q1[g], t2[g], g)
        send("ba", t2[g], q2[g], 20 + g)

    gain = jnp.sum(skip_all[:, 0, :] * lift_ref[...], 1, keepdims=True)

    def skip_piece(n):
        part = pl.ds(pl.multiple_of(512 * n, 512), 512)
        for pair in range(2):
            rows = slice(16 * pair, 16 * pair + 16)
            total = jnp.zeros((16, 512), F32)
            for c in range(C):
                total = total + g0[c, rows, part].astype(F32) * gain[c : c + 1, :]
            out_ref[rows, part] = total

    loop(4, skip_piece)

    for g in range(NG):
        arrive("ba", q2[g], 20 + g)
        forward_y(q2[g], g)
        rows = slice(START[g], START[g] + 8)
        for k in range(3):
            w_re, w_im = weff[k, 0, rows, :], weff[k, 1, rows, :]
            s_re, s_im = sm[k, 0, g], sm[k, 1, g]
            fold[k] += w_re * s_re + w_im * s_im
            fold[3 + k] += w_re * s_im - w_im * s_re

    for i in range(6):
        fa[i : i + 1] = jnp.sum(fold[i], 0, keepdims=True)
    fa[6:8] = jnp.zeros((2, 512), F32)
    for m in range(18):
        value = tile_of(lambda t: fa[:, 128 * t : 128 * t + 128], m)
        shift = (-24 * m) % 128
        vv[8 * m : 8 * m + 8] = pltpu.roll(value, shift, 1) if shift else value
    for p in range(2):
        parts = []
        for k in range(3):
            value = vv[pl.ds(3 * p + k, 18, stride=8), :]
            parts.append(pltpu.roll(value, 24 * k, 1) if k else value)
        full = jnp.where(lanes(18) < 24, parts[0], jnp.where(lanes(18) < 48, parts[1], parts[2]))
        mt0[pl.ds(p, 18, stride=2), :] = full
    values = mt0[...].astype(BF)
    out = dot_nt(yb_ref[0], values) - swap(dot_nt(yb_ref[1], values))
    t3[...] = out.astype(BF).reshape(NB, 32, 128)
    send("ba", t3, q3, 24)
    arrive("ba", q3, 24)
    t4[...] = back_x(q3[...].reshape(256, 128)).astype(BF).reshape(NA, 32, 128)
    send("aa", t4, q4, 25)
    load_signs.wait()
    arrive("aa", q4, 25)
    for t in range(6):
        part = slice(128 * t, 128 * t + 128)
        full = None
        for j in range(3 if t < 5 else 1):
            value = q4[3 * t + j].astype(F32)
            if j:
                value = jnp.where(lanes(32) < LM * j, full, pltpu.roll(value, LM * j, 1))
            full = value
        turned = swap(full)
        for i in range(4):
            variant = (turned if i == 3 else full) * signs[i : i + 1, part]
            bx0[32 * i : 32 * i + 32, part] = variant.astype(BF)
    quarter = dot_nt(bx0[...], plane[0:512, :]) * SCALE_ZT
    even, half, odd, turn = [quarter[32 * i : 32 * i + 32] for i in range(4)]
    out_ref[:, 0:512] += even + odd
    out_ref[:, 512:1024] += half + turn
    out_ref[:, 1024:1536] += even - odd
    out_ref[:, 1536:2048] += half - turn

    for g in range(NG):
        drain("aa", s1[g], g)
        drain("ba", s2[g], 4 + g)
        drain("ba", s3[g], 8 + g)
        drain("aa", s4[g], 12 + g)
        drain("aa", t1[g], 16 + g)
        drain("ba", t2[g], 20 + g)
    drain("ba", t3, 24)
    drain("aa", t4, 25)


def per_device(cotangent, pre_activations, spectral_weights, skip_weights, lift_weights):
    bf = lambda table: jnp.asarray(table.astype(np.float32), dtype=BF)
    forward_x_table = x_table()
    back_x_table = forward_x_table.transpose(0, 2, 1) / 64
    any_spec = pl.BlockSpec(memory_space=pl.ANY)
    kinds = [NA, NA, NB, NB, NB, NB, NA, NA, NA, NA, NB, NB]
    scratch = [
        pltpu.VMEM((C, 4, 8, NZT), BF),
        pltpu.VMEM((2, C, 4, 8, NZT), BF),
        pltpu.VMEM((2, C, C, 3, 2, 432), BF),
        pltpu.VMEM((C, 2, C), BF),
        pltpu.VMEM((1, C), F32),
        pltpu.VMEM((NZT, 768), BF),
        pltpu.VMEM((2, 256, 512), BF),
        pltpu.VMEM((2, 512, 256), BF),
        pltpu.VMEM((2, 80, 256), BF),
        pltpu.VMEM((2, 256, 128), BF),
        pltpu.VMEM((8, 768), F32),
        pltpu.VMEM((C, 32, NZT), BF),
        pltpu.VMEM((C, 32, NZT), BF),
        pltpu.VMEM((C, 32, NZT), F32),
        pltpu.VMEM((C, 32, NZT), F32),
        pltpu.VMEM((224, 768), BF),
        pltpu.VMEM((320, 320), BF),
        pltpu.VMEM((C, 3, 40, 432), F32),
        *[pltpu.VMEM((2, size, 32, 128), BF) for size in kinds],
        *[pltpu.VMEM((2, size, 32, 256), BF) for size in kinds],
        pltpu.VMEM((NB, 32, 128), BF), pltpu.VMEM((NB, 32, 128), BF),
        pltpu.VMEM((NA, 32, 128), BF), pltpu.VMEM((NA, 32, 128), BF),
        pltpu.VMEM((296, 128), F32),
        pltpu.VMEM((3, 2, NG, 8, 512), F32),
        pltpu.VMEM((3, 2, 4, 56, 128), F32),
        pltpu.VMEM((3, 2, 8, 512), F32),
        pltpu.VMEM((296, 128), F32),
        pltpu.VMEM((3, 2, 32, 512), F32),
        pltpu.VMEM((6, 8, 512), F32),
        pltpu.VMEM((8, 512), F32),
        pltpu.VMEM((144, 128), F32),
        pltpu.VMEM((128, 128), F32),
        pltpu.VMEM((128, 768), BF),
        pltpu.VMEM((C, 2, 128), F32),
        pltpu.SemaphoreType.DMA((19,)),
        pltpu.SemaphoreType.DMA((26,)),
        pltpu.SemaphoreType.DMA((26,)),
    ]
    out = pl.pallas_call(
        kernel,
        out_shape=jax.ShapeDtypeStruct((32, NZT), F32),
        in_specs=[any_spec] * 11,
        out_specs=pl.BlockSpec(memory_space=pltpu.VMEM),
        scratch_shapes=scratch,
        compiler_params=pltpu.CompilerParams(
            collective_id=0, has_side_effects=True, vmem_limit_bytes=66000000
        ),
        name="fno_grad",
    )(
        cotangent.reshape(C, 4, 8, NZT),
        pre_activations.reshape(2, C, 4, 8, NZT),
        spectral_weights.transpose(0, 2, 3, 4, 1, 5),
        skip_weights.transpose(1, 0, 2),
        lift_weights.reshape(1, C),
        bf(plane_table()),
        bf(forward_x_table),
        bf(back_x_table),
        bf(y_table()),
        bf(y_back_table()),
        jnp.asarray(quarter_signs(), F32),
    )
    return out.reshape(1, 4, 8, NZT)


def solution(mesh):
    return jax.shard_map(
        per_device,
        mesh=mesh,
        in_specs=(
            P(None, None, "aa", "ba", None),
            P(None, None, None, "aa", "ba", None),
            P(None, None, None, None, "ba", "aa"),
            P(),
            P(),
        ),
        out_specs=P(None, "aa", "ba", None),
        check_vma=False,
    )
```

time: 73.7 us -> 71.5 us (0.970)
  Pallas kernels: 71.9 us -> 69.7 us
    pallas_call x1, Pallas kernels: 71.9 us -> 69.7 us  [per_device(): pl.pallas_call(kernel, out_shape=jax.ShapeDtypeStruct((32, NZT), F32), in...]
where the time goes in v2:
time: 71.5 us; the launch traced here: 71.3 us
  Pallas kernels  69.7 us (97%)
  local copies, waits for them, and re-layouts  1.67 us (2%)
    pallas_call x1, Pallas kernels, per_device(): pl.pallas_call(kernel, out_shape=jax.ShapeDtypeStruct((32, NZT), F32), in...  69.7 us
    unnamed x1, local copies, waits for them, and re-layouts  1.67 us

profile of v2, /device:TPU:1, one launch (start us, length us, event | category | flops | bytes accessed | tf_op | source)
XLA Modules:
  0.0 71.3 jit_solution(1854318196228082094)
XLA Ops:
  0.0 69.7 %fno_grad.1 = f32[32,2048]{1,0:T(8,128)} custom-call(bf16[20,4,8,2048]{3,2,1,0:T(8,128)(2,1)} %bitcast.8, bf16[2,20,4,8,2048]{4,3,2,1,0:T(8,128)(2,1)} %bitcast.6, bf16[2,20,20,3,2,432]{5,4,3,2,1,0:T(2,128)(2,1)} %bitcast.7, bf16[20,2,20]{2,1,0:T(2,128)(2,1)} %bitcast.10, f32[1,20]{1,0:T(1,128)} %bitcast.11, bf16[2048,768]{1,0:T(8,128)(2,1)} %constant.12.clone.plane_h, ...), custom_call_target="tpu_custom_call" | custom-call | tf_op jit(solution)/shard_map/fno_grad/pallas_call | solution.py:597
  69.7 1.7 %copy.13 = f32[1,4,8,2048]{3,2,1,0:T(8,128)} copy(f32[1,4,8,2048]{3,2,1,0:T(8,128)} %bitcast.9) | data formatting | bytes 524288

commit v3 on v2

--- a/solution.py
+++ b/solution.py
@@ -30,18 +30,36 @@
 
 
 def plane_table():
-    joint = np.arange(24 * 12)
-    kz = freq(24)[joint // 12]
-    kt = joint % 12
-    cell = np.arange(NZT)
-    turns = (kz[None, :] * (cell[:, None] // 32) * 32 + kt[None, :] * (cell[:, None] % 32) * 64) % NZT
-    angle = 2.0 * np.pi / NZT * turns
-    table = np.zeros((NZT, 768))
-    owner, local = joint // 18, joint % 18
-    column = 128 * (owner // 3) + LM * (owner % 3) + 2 * local
-    table[:, column] = np.cos(angle)
-    table[:, column + 1] = -np.sin(angle)
+    cell = np.arange(512)
+    kt = np.arange(12)
+    table = np.zeros((6, 512, 256))
+    for f in range(24):
+        kz, rest, place = freq(24)[f], f % 4, f // 4
+        column = (24 * place if place < 5 else 128) + 2 * kt
+        turns = (kz * (cell[:, None] // 32) * 32 + kt[None, :] * (cell[:, None] % 32) * 64) % NZT
+        angle = 2.0 * np.pi / NZT * turns
+        index = {0: 0, 2: 1, 1: 2, 3: 3}[rest]
+        table[index][:, column] = np.cos(angle)
+        table[index][:, column + 1] = -np.sin(angle)
+        if rest % 2:
+            sign = -1 if rest == 1 else 1
+            table[index + 2][:, column] = sign * np.sin(angle)
+            table[index + 2][:, column + 1] = sign * np.cos(angle)
     return table
+
+
+CLASS = (0, 2, 1, 3)
+
+
+def slot(f):
+    return 24 * (f // 4) if f < 20 else 128
+
+
+def pieces_of(a):
+    u = a // 2
+    if a % 2 == 0:
+        return [(3 * u, 0, 24, 0), (3 * u + 1, 0, 12, 24)]
+    return [(3 * u + 1, 12, 12, 0), (3 * u + 2, 0, 24, 12)]
 
 
 def line_angle():
@@ -72,20 +90,6 @@
     return wide
 
 
-def quarter_signs():
-    joint = np.arange(24 * 12)
-    rest = freq(24)[joint // 12] % 4
-    owner, local = joint // 18, joint % 18
-    column = 128 * (owner // 3) + LM * (owner % 3) + 2 * local
-    table = np.zeros((8, 768))
-    for part in range(2):
-        table[0, column + part] = rest % 2 == 0
-        table[1, column + part] = np.where(rest % 2 == 0, 1 - rest, 0)
-        table[2, column + part] = rest % 2
-        table[3, column + part] = np.where(rest % 2 == 1, rest - 2, 0)
-    return table
-
-
 def swap(values):
     even = lax.broadcasted_iota(jnp.int32, (values.shape[0], 128), 1) % 2 == 0
     parts = []
@@ -113,13 +117,13 @@
 
 
 def kernel(
-    cot_h, pre_h, wts_h, skip_h, lift_h, plane_h, xf_h, xb_h, yf_h, yb_h, signs_h, out_ref,
-    cot, pre, wts, skip_ref, lift_ref, plane, xf, xb, yf_ref, yb_ref, signs,
-    g1, g0, slope0, skip1, bx, kron, wide,
+    cot_h, pre_h, wts_h, skip_h, lift_h, plane_h, xf_h, xb_h, yf_h, yb_h, out_ref,
+    cot, pre, wts, skip_ref, lift_ref, plane, xf, xb, yf_ref, yb_ref,
+    g1, g0, slope0, skip1, bx, pz, kron, wide,
     s1n, r1n, s2n, r2n, s3n, r3n, s4n, r4n, t1n, q1n, t2n, q2n,
     s1w, r1w, s2w, r2w, s3w, r3w, s4w, r4w, t1w, q1w, t2w, q2w,
     t3, q3, t4, q4,
-    q, sm, mm, mg, mt, weff, fold, fa, vv, mt0, bx0, lift_rows,
+    q, sm, mm, mg, mt, weff, fold, lifted, lift_rows,
     in_sem, send_sem, recv_sem,
 ):
     me_a = lax.axis_index("aa")
@@ -152,7 +156,6 @@
     load_yb = pltpu.make_async_copy(yb_h, yb_ref, in_sem.at[15])
     load_skip = pltpu.make_async_copy(skip_h, skip_ref, in_sem.at[16])
     load_lift = pltpu.make_async_copy(lift_h, lift_ref, in_sem.at[17])
-    load_signs = pltpu.make_async_copy(signs_h, signs, in_sem.at[18])
     loads[0].start()
     loads[1].start()
     load_plane.start()
@@ -174,7 +177,6 @@
         box[..., 24:32, :] = jnp.zeros(box.shape[:-2] + (8, box.shape[-1]), BF)
     mm[...] = jnp.zeros(mm.shape, F32)
     mt[...] = jnp.zeros(mt.shape, F32)
-    mt0[...] = jnp.zeros(mt0.shape, F32)
     weff[...] = jnp.zeros(weff.shape, F32)
     fold[...] = jnp.zeros(fold.shape, F32)
     sm[...] = jnp.zeros(sm.shape, F32)
@@ -221,43 +223,58 @@
         part = span(axis, src)
         pltpu.make_async_copy(part, part, send_sem.at[slot]).wait()
 
-    def forward_zt(field, g, dst):
-        values = field[START[g] : START[g] + COUNT[g]].reshape(COUNT[g] * 32, NZT)
-        for block in range(3):
-            out = dot(values, plane[:, 256 * block : 256 * block + 256])
-            for a in range(6 * block, min(6 * block + 6, NA)):
-                t, j = a // 3 - 2 * block, a % 3
-                low = high = None
-                for c in range(COUNT[g]):
-                    piece = out[32 * c : 32 * c + 32, 128 * t : 128 * t + 128]
-                    shift = (LM * c - LM * j) % 128
+    def combine(fields, rows, part):
+        sum02, sum13 = fields[0] + fields[2], fields[1] + fields[3]
+        pz[0, rows, part] = (sum02 + sum13).astype(BF)
+        pz[1, rows, part] = (sum02 - sum13).astype(BF)
+        pz[2, rows, part] = (fields[0] - fields[2]).astype(BF)
+        pz[3, rows, part] = (fields[1] - fields[3]).astype(BF)
+
+    def forward_zt(g, dst):
+        rows = slice(0, 32 * COUNT[g])
+        odd, turned = pz[2, rows], pz[3, rows]
+        out = [
+            dot(pz[0, rows], plane[0]),
+            dot(pz[1, rows], plane[1]),
+            dot(odd, plane[2]) + dot(turned, plane[4]),
+            dot(odd, plane[3]) + dot(turned, plane[5]),
+        ]
+        for a in range(NA):
+            low = high = None
+            for c in range(COUNT[g]):
+                for f, first, size, place in pieces_of(a):
+                    t, source = divmod(slot(f) + first, 128)
+                    start = LM * c + place
+                    piece = out[CLASS.index(f % 4)][32 * c : 32 * c + 32, 128 * t : 128 * t + 128]
+                    shift = (start - source) % 128
                     if shift:
                         piece = pltpu.roll(piece, shift, 1)
-                    start = LM * c
                     if start < 128:
                         low = piece if low is None else jnp.where(lanes(32) < start, low, piece)
-                    if start + LM > 128:
+                    if start + size > 128:
                         high = piece if high is None else jnp.where(lanes(32) < start - 128, high, piece)
-                dst[a, :, 0:128] = low.astype(BF)
-                if high is not None:
-                    dst[a, :, 128:256] = high.astype(BF)
+            dst[a, :, 0:128] = low.astype(BF)
+            if high is not None:
+                dst[a, :, 128:256] = high.astype(BF)
 
     def forward_x(src, dst, g):
         values = src[...].reshape(512, WIDTH[g])
         out = dot(xf[0], values) + swap(dot(xf[1], values))
         dst[...] = out.astype(BF).reshape(NB, 32, WIDTH[g])
 
+    def spectrum_y(src, g):
+        values = src[...].reshape(256, WIDTH[g])
+        return dot(yf_ref[0], values) + swap(dot(yf_ref[1], values))
+
     def forward_y(src, g):
         size = WIDTH[g]
-        values = src[...].reshape(256, size)
-        out = dot(yf_ref[0], values) + swap(dot(yf_ref[1], values))
+        out = spectrum_y(src, g)
         full = jnp.concatenate([out, jnp.zeros((48, size), F32)], 0)
         q[0:size] = full.T
         for p in range(2):
             tiles = [[None] * 4 for _ in range(3)]
             for m in range(18):
                 rows = q[pl.ds(2 * m + p, 8, stride=LM), :]
-                rows = jnp.where(row8 < COUNT[g], rows, 0.0)
                 t, off = divmod(24 * m, 128)
                 for k in range(3):
                     shift = (24 * m - 24 * k) % 128
@@ -321,31 +338,50 @@
         turned = -swap(values.astype(F32))
         return dot(xb[0], values) + dot(xb[1], turned.astype(BF))
 
-    def unpack(src, g):
-        for c in range(COUNT[g]):
-            start = LM * c
-            low = start // 128
-            for t in range(6):
-                full = None
-                for j in range(3 if t < 5 else 1):
-                    a = 3 * t + j
-                    value = src[a, :, 128 * low : 128 * low + 128].astype(F32)
-                    if start % 128 + LM > 128:
-                        value = jnp.where(lanes(32) < 64, src[a, :, 128:256].astype(F32), value)
-                    shift = (LM * j - start) % 128
-                    value = pltpu.roll(value, shift, 1) if shift else value
-                    full = value if full is None else jnp.where(lanes(32) < LM * j, full, value)
-                bx[32 * c : 32 * c + 32, 128 * t : 128 * t + 128] = full.astype(BF)
+    def unpack(src, count):
+        for c in range(count):
+            for r in range(4):
+                for t in range(2):
+                    full = None
+                    for f in [r, 4 + r, 8 + r, 12 + r, 16 + r] if t == 0 else [20 + r]:
+                        for a in (f // 3 * 2, f // 3 * 2 + 1):
+                            for kz, first, size, place in pieces_of(a):
+                                if kz != f:
+                                    continue
+                                low, source = divmod(LM * c + place, 128)
+                                value = src[a, :, 128 * low : 128 * low + 128].astype(F32)
+                                if source + size > 128:
+                                    value = jnp.where(lanes(32) < 64, src[a, :, 128:256].astype(F32), value)
+                                start = (slot(f) + first) % 128
+                                shift = (start - source) % 128
+                                value = pltpu.roll(value, shift, 1) if shift else value
+                                full = value if full is None else jnp.where(lanes(32) < start, full, value)
+                    bx[CLASS.index(r), 32 * c : 32 * c + 32, 128 * t : 128 * t + 128] = full.astype(BF)
+
+    def inverse_zt(count, h):
+        rows, part = slice(0, 32 * count), slice(256 * h, 256 * h + 256)
+        even = dot_nt(bx[0, rows], plane[0, part])
+        half = dot_nt(bx[1, rows], plane[1, part])
+        odd = dot_nt(bx[2, rows], plane[2, part]) + dot_nt(bx[3, rows], plane[3, part])
+        turn = dot_nt(bx[2, rows], plane[4, part]) + dot_nt(bx[3, rows], plane[5, part])
+        total, rest = even + half, even - half
+        return [total + odd, rest + turn, total - odd, rest - turn]
 
     def grad_top(g):
         def one(i):
             c = START[g] + i
             for pair in range(2):
-                for n in range(4):
-                    part = slice(512 * n, 512 * n + 512)
-                    v = pre[1, c, 2 * pair : 2 * pair + 2, :, part].astype(F32).reshape(16, 512)
-                    d = cot[c, 2 * pair : 2 * pair + 2, :, part].astype(F32).reshape(16, 512)
-                    g1[c, 16 * pair : 16 * pair + 16, part] = (d * slope_of(v)).astype(BF)
+                for h in range(4):
+                    fields = []
+                    for n in range(4):
+                        part = slice(512 * n + 128 * h, 512 * n + 128 * h + 128)
+                        v = pre[1, c, 2 * pair : 2 * pair + 2, :, part].astype(F32).reshape(16, 128)
+                        d = cot[c, 2 * pair : 2 * pair + 2, :, part].astype(F32).reshape(16, 128)
+                        value = (d * slope_of(v)).astype(BF)
+                        g1[c, 16 * pair : 16 * pair + 16, part] = value
+                        fields.append(value.astype(F32))
+                    rows = pl.ds(pl.multiple_of(32 * i + 16 * pair, 16), 16)
+                    combine(fields, rows, slice(128 * h, 128 * h + 128))
 
         loop(COUNT[g], one)
 
@@ -358,10 +394,10 @@
         grad_top(g)
         if g == 0:
             load_plane.wait()
-            late = [load_skip, load_w1, load_xf, load_yf, load_yb, load_xb, load_lift, load_w0, load_pre0, load_signs]
+            late = [load_skip, load_w1, load_xf, load_yf, load_yb, load_xb, load_lift, load_w0, load_pre0]
             for copy in loads[4:] + late:
                 copy.start()
-        forward_zt(g1, g, s1[g])
+        forward_zt(g, s1[g])
         if g == 0:
             pl.semaphore_wait(barrier, NA + NB - 2)
         send("aa", s1[g], r1[g], g)
@@ -453,19 +489,37 @@
     loop(C, slope_one)
 
     for g in range(NG):
+        size = WIDTH[g]
+        rows = slice(START[g], START[g] + 8)
+        for m in range(18):
+            for p in range(2):
+                parts = []
+                for k in range(3):
+                    value = tile_of(lambda t: weff[k, p, rows, 128 * t : 128 * t + 128], m)
+                    shift = (24 * k - 24 * m) % 128
+                    parts.append(pltpu.roll(value, shift, 1) if shift else value)
+                row = jnp.where(lane < 24, parts[0], jnp.where(lane < 48, parts[1], parts[2]))
+                mt[pl.ds(2 * m + p, 8, stride=LM), :] = jnp.where(row8 < COUNT[g], row, 0.0)
+        turned = mt[0:size].T[0:80]
+        lifted[g, 0, :, 0:size] = turned
+        lifted[g, 1, :, 0:size] = -swap(turned)
+
+    for g in range(NG):
         arrive("aa", r4[g], 12 + g)
-        unpack(r4[g], g)
-
-        def piece(n):
-            part = pl.ds(pl.multiple_of(512 * n, 512), 512)
-            spectral = dot_nt(bx[0 : 32 * COUNT[g]], plane[part, :]).reshape(COUNT[g], 32, 512)
+        unpack(r4[g], COUNT[g])
+        for h in range(2):
+            shifts = inverse_zt(COUNT[g], h)
             for c in range(COUNT[g]):
                 o = START[g] + c
-                incoming = skip1[o, :, part] + spectral[c] * SCALE_ZT
-                g0[o, :, part] = (incoming * slope0[o, :, part]).astype(BF)
-
-        loop(4, piece)
-        forward_zt(g0, g, t1[g])
+                fields = []
+                for n in range(4):
+                    part = slice(512 * n + 256 * h, 512 * n + 256 * h + 256)
+                    incoming = skip1[o, :, part] + shifts[n][32 * c : 32 * c + 32] * SCALE_ZT
+                    value = (incoming * slope0[o, :, part]).astype(BF)
+                    g0[o, :, part] = value
+                    fields.append(value.astype(F32))
+                combine(fields, slice(32 * c, 32 * c + 32), slice(256 * h, 256 * h + 256))
+        forward_zt(g, t1[g])
         send("aa", t1[g], q1[g], 16 + g)
 
     for g in range(NG):
@@ -488,55 +542,35 @@
 
     for g in range(NG):
         arrive("ba", q2[g], 20 + g)
-        forward_y(q2[g], g)
-        rows = slice(START[g], START[g] + 8)
-        for k in range(3):
-            w_re, w_im = weff[k, 0, rows, :], weff[k, 1, rows, :]
-            s_re, s_im = sm[k, 0, g], sm[k, 1, g]
-            fold[k] += w_re * s_re + w_im * s_im
-            fold[3 + k] += w_re * s_im - w_im * s_re
-
-    for i in range(6):
-        fa[i : i + 1] = jnp.sum(fold[i], 0, keepdims=True)
-    fa[6:8] = jnp.zeros((2, 512), F32)
-    for m in range(18):
-        value = tile_of(lambda t: fa[:, 128 * t : 128 * t + 128], m)
-        shift = (-24 * m) % 128
-        vv[8 * m : 8 * m + 8] = pltpu.roll(value, shift, 1) if shift else value
-    for p in range(2):
-        parts = []
-        for k in range(3):
-            value = vv[pl.ds(3 * p + k, 18, stride=8), :]
-            parts.append(pltpu.roll(value, 24 * k, 1) if k else value)
-        full = jnp.where(lanes(18) < 24, parts[0], jnp.where(lanes(18) < 48, parts[1], parts[2]))
-        mt0[pl.ds(p, 18, stride=2), :] = full
-    values = mt0[...].astype(BF)
-    out = dot_nt(yb_ref[0], values) - swap(dot_nt(yb_ref[1], values))
+        part = slice(0, WIDTH[g])
+        out = spectrum_y(q2[g], g)
+        fold[0, :, part] += out * lifted[g, 0, :, part]
+        fold[1, :, part] += out * lifted[g, 1, :, part]
+
+    pairs = []
+    for t in range(2):
+        real, imag = fold[0, :, 128 * t : 128 * t + 128], fold[1, :, 128 * t : 128 * t + 128]
+        real = real + pltpu.roll(real, 127, 1)
+        imag = imag + pltpu.roll(imag, 1, 1)
+        pairs.append(jnp.where(lanes(80) % 2 == 0, real, imag))
+    total = pairs[0]
+    for c in range(1, 7):
+        value = pairs[0] if LM * c + LM <= 128 else pairs[1]
+        if c == 3:
+            value = jnp.where(lanes(80) < 64, pairs[1], pairs[0])
+        total = total + pltpu.roll(value, (-LM * c) % 128, 1)
+    values = jnp.concatenate([total, jnp.zeros((48, 128), F32)], 0).astype(BF)
+    out = dot(yb_ref[0], values) - swap(dot(yb_ref[1], values))
     t3[...] = out.astype(BF).reshape(NB, 32, 128)
     send("ba", t3, q3, 24)
     arrive("ba", q3, 24)
     t4[...] = back_x(q3[...].reshape(256, 128)).astype(BF).reshape(NA, 32, 128)
     send("aa", t4, q4, 25)
-    load_signs.wait()
     arrive("aa", q4, 25)
-    for t in range(6):
-        part = slice(128 * t, 128 * t + 128)
-        full = None
-        for j in range(3 if t < 5 else 1):
-            value = q4[3 * t + j].astype(F32)
-            if j:
-                value = jnp.where(lanes(32) < LM * j, full, pltpu.roll(value, LM * j, 1))
-            full = value
-        turned = swap(full)
-        for i in range(4):
-            variant = (turned if i == 3 else full) * signs[i : i + 1, part]
-            bx0[32 * i : 32 * i + 32, part] = variant.astype(BF)
-    quarter = dot_nt(bx0[...], plane[0:512, :]) * SCALE_ZT
-    even, half, odd, turn = [quarter[32 * i : 32 * i + 32] for i in range(4)]
-    out_ref[:, 0:512] += even + odd
-    out_ref[:, 512:1024] += half + turn
-    out_ref[:, 1024:1536] += even - odd
-    out_ref[:, 1536:2048] += half - turn
+    unpack(q4, 1)
+    for h in range(2):
+        for n, value in enumerate(inverse_zt(1, h)):
+            out_ref[:, 512 * n + 256 * h : 512 * n + 256 * h + 256] += value * SCALE_ZT
 
     for g in range(NG):
         drain("aa", s1[g], g)
@@ -561,17 +595,17 @@
         pltpu.VMEM((2, C, C, 3, 2, 432), BF),
         pltpu.VMEM((C, 2, C), BF),
         pltpu.VMEM((1, C), F32),
-        pltpu.VMEM((NZT, 768), BF),
+        pltpu.VMEM((6, 512, 256), BF),
         pltpu.VMEM((2, 256, 512), BF),
         pltpu.VMEM((2, 512, 256), BF),
         pltpu.VMEM((2, 80, 256), BF),
         pltpu.VMEM((2, 256, 128), BF),
-        pltpu.VMEM((8, 768), F32),
         pltpu.VMEM((C, 32, NZT), BF),
         pltpu.VMEM((C, 32, NZT), BF),
         pltpu.VMEM((C, 32, NZT), F32),
         pltpu.VMEM((C, 32, NZT), F32),
-        pltpu.VMEM((224, 768), BF),
+        pltpu.VMEM((4, 224, 256), BF),
+        pltpu.VMEM((4, 224, 512), BF),
         pltpu.VMEM((320, 320), BF),
         pltpu.VMEM((C, 3, 40, 432), F32),
         *[pltpu.VMEM((2, size, 32, 128), BF) for size in kinds],
@@ -584,11 +618,8 @@
         pltpu.VMEM((3, 2, 8, 512), F32),
         pltpu.VMEM((296, 128), F32),
         pltpu.VMEM((3, 2, 32, 512), F32),
-        pltpu.VMEM((6, 8, 512), F32),
-        pltpu.VMEM((8, 512), F32),
-        pltpu.VMEM((144, 128), F32),
-        pltpu.VMEM((128, 128), F32),
-        pltpu.VMEM((128, 768), BF),
+        pltpu.VMEM((2, 80, 256), F32),
+        pltpu.VMEM((NG, 2, 80, 256), F32),
         pltpu.VMEM((C, 2, 128), F32),
         pltpu.SemaphoreType.DMA((19,)),
         pltpu.SemaphoreType.DMA((26,)),
@@ -597,7 +628,7 @@
     out = pl.pallas_call(
         kernel,
         out_shape=jax.ShapeDtypeStruct((32, NZT), F32),
-        in_specs=[any_spec] * 11,
+        in_specs=[any_spec] * 10,
         out_specs=pl.BlockSpec(memory_space=pltpu.VMEM),
         scratch_shapes=scratch,
         compiler_params=pltpu.CompilerParams(
@@ -615,7 +646,6 @@
         bf(back_x_table),
         bf(y_table()),
         bf(y_back_table()),
-        jnp.asarray(quarter_signs(), F32),
     )
     return out.reshape(1, 4, 8, NZT)
 

time: 71.5 us -> 70.3 us (0.983)
  Pallas kernels: 69.7 us -> 68.5 us
    pallas_call x1, Pallas kernels: 69.7 us -> 68.5 us  [per_device(): pl.pallas_call(kernel, out_shape=jax.ShapeDtypeStruct((32, NZT), F32), in...]
where the time goes in v3:
time: 70.3 us; the launch traced here: 70.2 us
  Pallas kernels  68.5 us (97%)
  local copies, waits for them, and re-layouts  1.67 us (2%)
    pallas_call x1, Pallas kernels, per_device(): pl.pallas_call(kernel, out_shape=jax.ShapeDtypeStruct((32, NZT), F32), in...  68.5 us
    unnamed x1, local copies, waits for them, and re-layouts  1.67 us

profile of v3, /device:TPU:1, one launch (start us, length us, event | category | flops | bytes accessed | tf_op | source)
XLA Modules:
  0.0 70.2 jit_solution(432595117748818816)
XLA Ops:
  0.0 68.5 %fno_grad.1 = f32[32,2048]{1,0:T(8,128)} custom-call(bf16[20,4,8,2048]{3,2,1,0:T(8,128)(2,1)} %bitcast.8, bf16[2,20,4,8,2048]{4,3,2,1,0:T(8,128)(2,1)} %bitcast.6, bf16[2,20,20,3,2,432]{5,4,3,2,1,0:T(2,128)(2,1)} %bitcast.7, bf16[20,2,20]{2,1,0:T(2,128)(2,1)} %bitcast.10, f32[1,20]{1,0:T(1,128)} %bitcast.11, bf16[6,512,256]{2,1,0:T(8,128)(2,1)} %constant.10.clone.plane_h, ...), custom_call_target="tpu_custom_call" | custom-call | tf_op jit(solution)/shard_map/fno_grad/pallas_call | solution.py:628
  68.5 1.7 %copy.12 = f32[1,4,8,2048]{3,2,1,0:T(8,128)} copy(f32[1,4,8,2048]{3,2,1,0:T(8,128)} %bitcast.9) | data formatting | bytes 524288

commit v4 on v3

--- a/solution.py
+++ b/solution.py
@@ -122,7 +122,7 @@
     g1, g0, slope0, skip1, bx, pz, kron, wide,
     s1n, r1n, s2n, r2n, s3n, r3n, s4n, r4n, t1n, q1n, t2n, q2n,
     s1w, r1w, s2w, r2w, s3w, r3w, s4w, r4w, t1w, q1w, t2w, q2w,
-    t3, q3, t4, q4,
+    t3, q3, t4, q4, q5,
     q, sm, mm, mg, mt, weff, fold, lifted, lift_rows,
     in_sem, send_sem, recv_sem,
 ):
@@ -198,7 +198,7 @@
 
     def send(axis, src, dst, slot):
         me = me_a if axis == "aa" else me_b
-        rows = pl.ds(0, 32 if axis == "aa" else 24)
+        rows = pl.ds(0, src.shape[1] if axis == "aa" else 24)
         for peer in partners(axis):
             pltpu.make_async_remote_copy(
                 src_ref=src.at[peer, rows],
@@ -564,10 +564,21 @@
     t3[...] = out.astype(BF).reshape(NB, 32, 128)
     send("ba", t3, q3, 24)
     arrive("ba", q3, 24)
-    t4[...] = back_x(q3[...].reshape(256, 128)).astype(BF).reshape(NA, 32, 128)
+    full = back_x(q3[...].reshape(256, 128)).reshape(NA, 4, 8, 128)
+    x0, x1, x2, x3 = [full[:, i].reshape(128, 128) for i in range(4)]
+    wide_lane = lanes(128)
+    x2 = pltpu.roll(x2, 2 * LM, 1)
+    x0 = jnp.where(wide_lane < LM, x0, jnp.where(wide_lane < 2 * LM, pltpu.roll(x1, LM, 1), x2))
+    t4[:, 0:8] = x0.astype(BF).reshape(NA, 8, 128)
+    t4[:, 8:16] = x3.astype(BF).reshape(NA, 8, 128)
     send("aa", t4, q4, 25)
     arrive("aa", q4, 25)
-    unpack(q4, 1)
+    shared = q4[:, 0:8].astype(F32).reshape(128, 128)
+    q5[:, 0:8] = shared.reshape(NA, 8, 128)
+    q5[:, 8:16] = pltpu.roll(shared, 128 - LM, 1).reshape(NA, 8, 128)
+    q5[:, 16:24] = pltpu.roll(shared, 128 - 2 * LM, 1).reshape(NA, 8, 128)
+    q5[:, 24:32] = q4[:, 8:16].astype(F32)
+    unpack(q5, 1)
     for h in range(2):
         for n, value in enumerate(inverse_zt(1, h)):
             out_ref[:, 512 * n + 256 * h : 512 * n + 256 * h + 256] += value * SCALE_ZT
@@ -611,7 +622,8 @@
         *[pltpu.VMEM((2, size, 32, 128), BF) for size in kinds],
         *[pltpu.VMEM((2, size, 32, 256), BF) for size in kinds],
         pltpu.VMEM((NB, 32, 128), BF), pltpu.VMEM((NB, 32, 128), BF),
-        pltpu.VMEM((NA, 32, 128), BF), pltpu.VMEM((NA, 32, 128), BF),
+        pltpu.VMEM((NA, 16, 128), BF), pltpu.VMEM((NA, 16, 128), BF),
+        pltpu.VMEM((NA, 32, 128), F32),
         pltpu.VMEM((296, 128), F32),
         pltpu.VMEM((3, 2, NG, 8, 512), F32),
         pltpu.VMEM((3, 2, 4, 56, 128), F32),

time: 70.3 us -> 70.5 us (level)
  no operation moved by 1% of the time
where the time goes in v4:
time: 70.5 us; the launch traced here: 70.3 us
  Pallas kernels  68.6 us (97%)
  local copies, waits for them, and re-layouts  1.67 us (2%)
    pallas_call x1, Pallas kernels, per_device(): pl.pallas_call(kernel, out_shape=jax.ShapeDtypeStruct((32, NZT), F32), in...  68.6 us
    unnamed x1, local copies, waits for them, and re-layouts  1.67 us

profile of v4, /device:TPU:1, one launch (start us, length us, event | category | flops | bytes accessed | tf_op | source)
XLA Modules:
  0.0 70.3 jit_solution(8044400112215116167)
XLA Ops:
  0.0 68.6 %fno_grad.1 = f32[32,2048]{1,0:T(8,128)} custom-call(bf16[20,4,8,2048]{3,2,1,0:T(8,128)(2,1)} %bitcast.8, bf16[2,20,4,8,2048]{4,3,2,1,0:T(8,128)(2,1)} %bitcast.6, bf16[2,20,20,3,2,432]{5,4,3,2,1,0:T(2,128)(2,1)} %bitcast.7, bf16[20,2,20]{2,1,0:T(2,128)(2,1)} %bitcast.10, f32[1,20]{1,0:T(1,128)} %bitcast.11, bf16[6,512,256]{2,1,0:T(8,128)(2,1)} %constant.10.clone.plane_h, ...), custom_call_target="tpu_custom_call" | custom-call | tf_op jit(solution)/shard_map/fno_grad/pallas_call | solution.py:640
  68.7 1.7 %copy.12 = f32[1,4,8,2048]{3,2,1,0:T(8,128)} copy(f32[1,4,8,2048]{3,2,1,0:T(8,128)} %bitcast.9) | data formatting | bytes 524288
